TPU v7x, 256 devices: a whole 4x4x8 slice. The times are simulated.
256 devices in a mesh: fsdp: 8 (over x, core), vocab: 32 (over y, z).
Axes of the slice: x: 4, y: 4, z: 8, core: 2. Of those that a mesh axis runs over, the one named last changes fastest.
Arguments:
- hidden_states: bfloat16 [1024, 3072], P('fsdp', 'vocab'), may hold values from -512 to 512
- head: bfloat16 [3072, 65536], P('fsdp', 'vocab'), may hold values from -0.25259074 to 0.25259074
- labels: int32 [1024], P('fsdp'), may hold values from 0 to 65535
Outputs:
- token_loss: float32 [1024], P('fsdp')
- state_grad: bfloat16 [1024, 3072], P('fsdp', 'vocab')
- head_grad: float32 [3072, 65536], P('fsdp', 'vocab')
All inputs are finite; a program needn't handle non-finite values.
Results may differ from a plain program's by a relative error of at most 0.0034.
Values may be sent and summed in bfloat16 or wider, within the bound.
A program may use at most 128 MiB of HBM per device.

v0:
```python
import jax
import jax.numpy as jnp
from jax import lax
from jax.sharding import PartitionSpec as P


def from_everyone(array, axis):
    peers = lax.axis_size(axis)
    return lax.all_to_all(
        jnp.broadcast_to(array[None], (peers, *array.shape)), axis, 0, 0, tiled=True
    )


def in_order(parts, dim):
    shape = list(parts.shape[1:])
    shape[dim] *= parts.shape[0]
    return jnp.moveaxis(parts, 0, dim).reshape(shape)


def collect(array, axis, dim):
    parts = from_everyone(array, axis)
    return in_order(parts, dim)


def all_in_one(array, axis):
    leaves = jax.tree.leaves(array)
    turns = sorted(range(len(leaves)), key=lambda k: -leaves[k].size)
    width = (1, *leaves[turns[0]].shape)[-1]
    lines = [
        jnp.pad(leaves[k].reshape(-1), (0, -leaves[k].size % width)).reshape(-1, width)
        for k in turns
    ]
    both, at, found = (from_everyone(jnp.concatenate(lines), axis), 0, {})
    for k, line in zip(turns, lines):
        section = both[:, at : at + len(line)].reshape(len(both), -1)
        found[k] = section[:, : leaves[k].size].reshape(-1, *leaves[k].shape)
        at += len(line)
    numbers = iter(range(len(leaves)))
    return jax.tree.map(lambda _: found[next(numbers)], array)


def combined_pairwise(pieces, combine):
    while len(jax.tree.leaves(pieces)[0]) > 1:
        pieces = jax.vmap(combine)(
            *(jax.tree.map(lambda part: part[side::2], pieces) for side in (0, 1))
        )
    return jax.tree.map(lambda part: part[0], pieces)


def joined_all(array, axis, combine):
    pieces = all_in_one(array, axis)
    return combined_pairwise(pieces, combine)


def cut_along(array, dim, peers):
    before, after = (array.shape[:dim], array.shape[dim + 1 :])
    return jnp.moveaxis(array.reshape(*before, peers, -1, *after), dim, 0)


def sum_at_owner(array, axis, dim):
    parts = cut_along(array, dim, lax.axis_size(axis))
    arrived = lax.all_to_all(parts, axis, split_axis=0, concat_axis=0, tiled=True)
    return arrived.sum(axis=0)


def combine_rows(first, second):
    peak = jnp.maximum(first[0], second[0])
    total = first[1] * jnp.exp(first[0] - peak) + second[1] * jnp.exp(second[0] - peak)
    return (peak, total, first[2] + second[2])


def local(hidden_states, head, labels):
    features = collect(hidden_states, "vocab", 1)
    weights = lax.all_gather(head, "fsdp", axis=0, tiled=True)
    logits = jnp.dot(features, weights, preferred_element_type=jnp.float32)
    width = weights.shape[1]
    columns = lax.axis_index("vocab") * width + jnp.arange(width, dtype=jnp.int32)
    hits = labels[:, None] == columns[None, :]
    local_target = jnp.sum(jnp.where(hits, logits, jnp.float32(0.0)), axis=1)
    local_peak = jnp.max(logits, axis=1)
    local_total = jnp.sum(jnp.exp(logits - local_peak[:, None]), axis=1)
    peak, total, target = joined_all((local_peak, local_total, local_target), "vocab", combine_rows)
    shifted = jnp.exp(logits - peak[:, None])
    token_loss = jnp.log(total) + peak - target
    errors = (shifted / total[:, None] - hits.astype(jnp.float32)).astype(jnp.bfloat16)
    state_terms = lax.dot_general(
        errors, weights, (((1,), (1,)), ((), ())), preferred_element_type=jnp.float32
    )
    state_grad = sum_at_owner(state_terms, "vocab", 1).astype(jnp.bfloat16)
    all_errors = lax.all_gather(errors, "fsdp", axis=0, tiled=True)
    slices = lax.all_to_all(features, "fsdp", split_axis=1, concat_axis=0, tiled=True)
    head_grad = lax.dot_general(
        slices, all_errors, (((0,), (0,)), ((), ())), preferred_element_type=jnp.float32
    )
    return (token_loss, state_grad, head_grad)


def solution(mesh):
    in_specs = (P("fsdp", "vocab"), P("fsdp", "vocab"), P("fsdp"))
    out_specs = (P("fsdp"), P("fsdp", "vocab"), P("fsdp", "vocab"))
    return jax.shard_map(local, mesh=mesh, in_specs=in_specs, out_specs=out_specs, check_vma=False)
```

profile of v0, /device:TPU:26, one launch (start us, length us, event | category | flops | bytes accessed | tf_op | source)
XLA Modules:
  0.0 188.6 jit_solution(7751389101750983921)
XLA Ops:
  7.2 0.0 all-gather.3.cloned.1.call-start
  7.2 0.7 all-gather.3.cloned.1.call-update
  7.9 1.7 broadcast_in_dim.8
  9.6 11.6 %all-to-all-start = ((bf16[32,128,96]{1,2,0:T(8,128)(2,1)}), bf16[32,128,96]{1,2,0:T(8,128)(2,1)}, u32[]{:S(2)}, u32[]{:S(2)}) async-start(bf16[32,128,96]{1,2,0:T(8,128)(2,1)} %broadcast_in_dim.8), calls=%async_computation | async-start | bytes 1572864 | tf_op jit(solution)/shard_map/all_to_all | solution.py:9
  21.2 0.0 all-gather.5.cloned.1.call-start
  21.3 21.1 %all-to-all-done = bf16[32,128,96]{1,2,0:T(8,128)(2,1)} async-done(((bf16[32,128,96]{1,2,0:T(8,128)(2,1)}), bf16[32,128,96]{1,2,0:T(8,128)(2,1)}, u32[]{:S(2)}, u32[]{:S(2)}) %all-to-all-start) | async-done | bytes 786464 | tf_op jit(solution)/shard_map/all_to_all | solution.py:9
  42.3 39.4 %all-gather.3.cloned.1.call-done = bf16[3072,2048]{1,0:T(8,128)(2,1)} async-done(((bf16[384,2048]{1,0:T(8,128)(2,1)}), bf16[3072,2048]{1,0:T(8,128)(2,1)}) %all-gather.3.cloned.1.call-update) | async-done | bytes 12582928 | tf_op jit(solution)/shard_map/all_gather | solution.py:74
  81.7 0.0 copy-start
  81.7 6.7 %fusion.4 = (f32[128]{0:T(128)S(1)}, f32[128,2048]{1,0:T(8,128)S(1)}) fusion(bf16[128,3072]{0,1:T(8,128)(2,1)} %bitcast.1, bf16[3072,2048]{1,0:T(8,128)(2,1)} %all-gather.3.cloned.1.call-done), kind=kOutput, calls=%fused_computation.17 | convolution fusion | flops 1610874752 | bytes 14418432 | tf_op jit(solution)/shard_map/dot_general | solution.py:75
  88.5 0.0 copy-done
  88.5 0.4 exponential_reduce_fusion
  88.9 18.1 %all_to_all.34 = f32[32,3,128]{2,1,0:T(4,128)S(1)} all-to-all(f32[32,3,128]{2,1,0:T(4,128)S(1)} %broadcast_in_dim.10), channel_id=1, replica_groups=mesh['fsdp'=8,'vocab'=32] {'vocab'}, dimensions={0} | all-to-all | bytes 98304 | tf_op jit(solution)/shard_map/all_to_all | solution.py:9
  107.5 0.5 bitcast_subtract_fusion
  108.1 1.2 fusion.2
  109.3 0.0 all-gather.5.cloned.1.call-update
  109.3 4.6 %all-to-all-start.3 = ((bf16[128,8,384]{0,2,1:T(8,128)(2,1)}), bf16[128,8,384]{0,2,1:T(8,128)(2,1)S(1)}, u32[]{:S(2)}, u32[]{:S(2)}) async-start(bf16[128,8,384]{0,2,1:T(8,128)(2,1)} %bitcast.13), calls=%async_computation.3 | async-start | bytes 1572864 | tf_op jit(solution)/shard_map/all_to_all | solution.py:91
  113.9 9.7 %fusion.5 = f32[128,3072]{0,1:T(8,128)} fusion(bf16[128,2048]{1,0:T(8,128)(2,1)} %fusion.2, bf16[3072,2048]{1,0:T(8,128)(2,1)} %all-gather.3.cloned.1.call-done), kind=kOutput, calls=%fused_computation.18 | convolution fusion | flops 1610612736 | bytes 14680064 | tf_op jit(solution)/shard_map/dot_general | solution.py:86
  123.6 6.8 %all-to-all-done.3 = bf16[128,8,384]{0,2,1:T(8,128)(2,1)S(1)} async-done(((bf16[128,8,384]{0,2,1:T(8,128)(2,1)}), bf16[128,8,384]{0,2,1:T(8,128)(2,1)S(1)}, u32[]{:S(2)}, u32[]{:S(2)}) %all-to-all-start.3) | async-done | bytes 786464 | tf_op jit(solution)/shard_map/all_to_all | solution.py:91
  130.4 7.4 %all-to-all-start.2 = ((f32[32,128,96]{1,2,0:T(8,128)}), f32[32,128,96]{1,2,0:T(8,128)S(1)}, u32[]{:S(2)}, u32[]{:S(2)}) async-start(f32[32,128,96]{1,2,0:T(8,128)} %bitcast.12), calls=%async_computation.2 | async-start | bytes 3145728 | tf_op jit(solution)/shard_map/all_to_all | solution.py:62
  137.8 1.2 copy.13
  139.0 35.0 %all-to-all-done.2 = f32[32,128,96]{1,2,0:T(8,128)S(1)} async-done(((f32[32,128,96]{1,2,0:T(8,128)}), f32[32,128,96]{1,2,0:T(8,128)S(1)}, u32[]{:S(2)}, u32[]{:S(2)}) %all-to-all-start.2) | async-done | bytes 1572896 | tf_op jit(solution)/shard_map/all_to_all | solution.py:62
  174.0 0.7 reduce_sum.29
  174.7 0.0 all-gather.5.cloned.1.call-done
  174.7 4.8 %convolution_bitcast_fusion = f32[384,2048]{0,1:T(8,128)S(1)} fusion(bf16[1024,2048]{1,0:T(8,128)(2,1)} %all-gather.5.cloned.1.call-done, bf16[1024,384]{1,0:T(8,128)(2,1)} %bitcast.35), kind=kOutput, calls=%fused_computation | convolution fusion | flops 1610612736 | bytes 8126464 | tf_op jit(solution)/shard_map/dot_general | solution.py:92
  179.4 2.4 %copy.14 = f32[384,2048]{1,0:T(8,128)} copy(f32[384,2048]{0,1:T(8,128)S(1)} %convolution_bitcast_fusion) | data formatting | bytes 6291456
  (36 shorter events, 0.5 us)
Async XLA Ops:
  7.2 74.6 %all-gather.3.cloned.1.call-start = ((), (), s32[]{:S(2)}) async-start(), calls=%async_computation.4 | async-start | bytes 14155776 | tf_op jit(solution)/shard_map/all_gather | solution.py:74
  9.6 32.7 %all-to-all-start = ((bf16[32,128,96]{1,2,0:T(8,128)(2,1)}), bf16[32,128,96]{1,2,0:T(8,128)(2,1)}, u32[]{:S(2)}, u32[]{:S(2)}) async-start(bf16[32,128,96]{1,2,0:T(8,128)(2,1)} %broadcast_in_dim.8), calls=%async_computation | async-start | bytes 1572864 | tf_op jit(solution)/shard_map/all_to_all | solution.py:9
  21.2 153.5 %all-gather.5.cloned.1.call-start = ((), (), s32[]{:S(2)}) async-start(), calls=%async_computation.5 | async-start | bytes 4718592 | tf_op jit(solution)/shard_map/all_gather | solution.py:90
  81.7 6.7 %copy-start = (s32[128]{0:T(128)S(1)}, s32[128]{0:T(128)}, u32[]{:S(2)}) copy-start(s32[128]{0:T(128)} %param.5) | copy-start | bytes 1540
  109.3 21.1 %all-to-all-start.3 = ((bf16[128,8,384]{0,2,1:T(8,128)(2,1)}), bf16[128,8,384]{0,2,1:T(8,128)(2,1)S(1)}, u32[]{:S(2)}, u32[]{:S(2)}) async-start(bf16[128,8,384]{0,2,1:T(8,128)(2,1)} %bitcast.13), calls=%async_computation.3 | async-start | bytes 1572864 | tf_op jit(solution)/shard_map/all_to_all | solution.py:91
  130.4 43.6 %all-to-all-start.2 = ((f32[32,128,96]{1,2,0:T(8,128)}), f32[32,128,96]{1,2,0:T(8,128)S(1)}, u32[]{:S(2)}, u32[]{:S(2)}) async-start(f32[32,128,96]{1,2,0:T(8,128)} %bitcast.12), calls=%async_computation.2 | async-start | bytes 3145728 | tf_op jit(solution)/shard_map/all_to_all | solution.py:62
Sparse Core Ops, SparseCore 0:
  9.8 71.8 all-gather.2
  109.4 33.9 all-gather.4
where the time goes:
time: 192 us; the launch traced here: 189 us
  waiting for transfers between devices  103 us (54%)
  starting transfers between devices  23.7 us (12%)
  matrix products  21.3 us (11%)
  blocking collectives  18.1 us (9%)
  between operations  14.2 us (7%)
  local copies, waits for them, and re-layouts  5.67 us (3%)
  other arithmetic  2.87 us (1%)
    all_gather x1, waiting for transfers between devices, local(): weights = lax.all_gather(head, 'fsdp', axis=0, tiled=True)  39.4 us
    all_to_all x1, waiting for transfers between devices, sum_at_owner(): lax.all_to_all(parts, axis, split_axis=0, concat_axis=0, tiled=True)  35 us
    all_to_all x1, waiting for transfers between devices, from_everyone(): lax.all_to_all(jnp.broadcast_to(array[None], (peers, *array.shape)), axis...  21.1 us
    all_to_all x1, blocking collectives, from_everyone(): lax.all_to_all(jnp.broadcast_to(array[None], (peers, *array.shape)), axis...  18.1 us
    all_to_all x1, starting transfers between devices, from_everyone(): lax.all_to_all(jnp.broadcast_to(array[None], (peers, *array.shape)), axis...  11.6 us
    dot_general x1, matrix products, local(): lax.dot_general(errors, weights, (((1,), (1,)), ((), ())), preferred_elem...  9.73 us
    all_to_all x1, starting transfers between devices, sum_at_owner(): lax.all_to_all(parts, axis, split_axis=0, concat_axis=0, tiled=True)  7.43 us
    all_to_all x1, waiting for transfers between devices, local(): lax.all_to_all(features, 'fsdp', split_axis=1, concat_axis=0, tiled=True)  6.77 us
  transfers between devices with their start and end apart: 5, of which 4 were waited for; matrix products, arithmetic and copies ran while one was open for 7% of the time, Pallas kernels for 0%

commit v1 on v0

v1 whole, which is shorter than its diff:
```python
import jax
import jax.numpy as jnp
from jax import lax
from jax.sharding import PartitionSpec as P


def combine(stats):
    peaks, totals, targets = stats[:, 0], stats[:, 1], stats[:, 2]
    peak = jnp.max(peaks, axis=0)
    total = jnp.sum(totals * jnp.exp(peaks - peak[None]), axis=0)
    return jnp.stack([peak, total, jnp.sum(targets, axis=0)])


def local(hidden_states, head, labels):
    fsdp, vocab = lax.axis_size("fsdp"), lax.axis_size("vocab")
    f, v = lax.axis_index("fsdp"), lax.axis_index("vocab")
    features, width = head.shape
    tokens = hidden_states.shape[0]
    share = width // fsdp
    states = lax.all_gather(hidden_states.T, "fsdp", axis=1, tiled=True)
    states = lax.all_gather(states, "vocab", axis=0, tiled=True)
    wanted = lax.all_gather(labels, "fsdp", axis=0, tiled=True)
    weights = lax.all_to_all(head, "fsdp", split_axis=1, concat_axis=0, tiled=True)
    logits = lax.dot_general(weights, states, (((0,), (0,)), ((), ())), preferred_element_type=jnp.float32)
    rows = v * width + f * share + jnp.arange(share, dtype=jnp.int32)
    hits = rows[:, None] == wanted[None, :]
    local_target = jnp.sum(jnp.where(hits, logits, jnp.float32(0.0)), axis=0)
    local_peak = jnp.max(logits, axis=0)
    local_total = jnp.sum(jnp.exp(logits - local_peak[None, :]), axis=0)
    stats = jnp.stack([local_peak, local_total, local_target])
    stats = combine(lax.all_gather(stats, "fsdp", axis=0))
    stats = combine(lax.all_gather(stats, "vocab", axis=0))
    peak, total, target = stats[0], stats[1], stats[2]
    loss = jnp.log(total) + peak - target
    token_loss = lax.dynamic_slice_in_dim(loss, f * tokens, tokens)
    errors = (jnp.exp(logits - peak[None, :]) / total[None, :] - hits.astype(jnp.float32)).astype(jnp.bfloat16)
    errors = lax.all_gather(errors, "fsdp", axis=0, tiled=True)
    terms = jnp.dot(head, errors, preferred_element_type=jnp.float32)
    parts = vocab // fsdp
    piece = features // parts
    terms = terms.reshape(parts, piece, fsdp, tokens).transpose(2, 0, 1, 3).reshape(vocab, piece, tokens)
    summed = lax.psum_scatter(terms, "vocab", scatter_dimension=0, tiled=False).astype(jnp.bfloat16)
    moves = [
        (a * vocab + u, (u // parts) * vocab + parts * a + u % parts)
        for a in range(fsdp)
        for u in range(vocab)
    ]
    state_grad = lax.ppermute(summed, ("fsdp", "vocab"), moves).T
    mine = lax.dynamic_slice_in_dim(states, f * features, features)
    head_grad = lax.dot_general(mine, errors, (((1,), (1,)), ((), ())), preferred_element_type=jnp.float32)
    return (token_loss, state_grad, head_grad)


def solution(mesh):
    in_specs = (P("fsdp", "vocab"), P("fsdp", "vocab"), P("fsdp"))
    out_specs = (P("fsdp"), P("fsdp", "vocab"), P("fsdp", "vocab"))
    return jax.shard_map(local, mesh=mesh, in_specs=in_specs, out_specs=out_specs, check_vma=False)
```

time: 192 us -> 459 us (2.39)
  waiting for transfers between devices: 103 us -> 309 us
  blocking collectives: 18.1 us -> 96.8 us
  starting transfers between devices: 23.7 us -> 9.34 us
  matrix products: 21.3 us -> 15.1 us
    reduce_scatter x0 -> x1, waiting for transfers between devices: none -> 218 us  [local(): lax.psum_scatter(terms, 'vocab', scatter_dimension=0, tiled=False)]
    all_gather x0 -> x4, blocking collectives: none -> 96.8 us  [the longest x1 48.6 us: local(): stats = combine(lax.all_gather(stats, 'vocab', axis=0))]
    all_to_all x3 -> x1, waiting for transfers between devices: 62.8 us -> 0.01 us  [local(): lax.all_to_all(head, 'fsdp', split_axis=1, concat_axis=0, tiled=True)]
    all_gather x2, waiting for transfers between devices: 39.4 us -> 90.7 us  [the longest x1 58.4 us: local(): states = lax.all_gather(states, 'vocab', axis=0, tiled=True)]
    all_to_all x3 -> x1, starting transfers between devices: 23.6 us -> 4.45 us  [local(): lax.all_to_all(head, 'fsdp', split_axis=1, concat_axis=0, tiled=True)]
    all_to_all x1 -> x0, blocking collectives: 18.1 us -> none  [from_everyone(): lax.all_to_all(jnp.broadcast_to(array[None], (peers, *array.shape)), axis...]
    dot_general x3, matrix products: 21.3 us -> 15.1 us  [the longest x1 5.93 us: local(): lax.dot_general(mine, errors, (((1,), (1,)), ((), ())), preferred_element...]
    ppermute x0 -> x1, starting transfers between devices: none -> 4.81 us  [local(): state_grad = lax.ppermute(summed, ('fsdp', 'vocab'), moves).T]
  transfers between devices with their start and end apart: 5 -> 5, of which waited for: 4 -> 3; matrix products, arithmetic and copies ran while one was open for 7% -> 2% of each run, Pallas kernels for 0% -> 0%
where the time goes in v1:
time: 459 us; the launch traced here: 454 us
  waiting for transfers between devices  309 us (67%)
  blocking collectives  96.8 us (21%)
  matrix products  15.1 us (3%)
  between operations  13.8 us (3%)
  starting transfers between devices  9.34 us (2%)
  local copies, waits for them, and re-layouts  6.86 us (1%)
    reduce_scatter x1, waiting for transfers between devices, local(): lax.psum_scatter(terms, 'vocab', scatter_dimension=0, tiled=False)  218 us
    all_gather x1, waiting for transfers between devices, local(): states = lax.all_gather(states, 'vocab', axis=0, tiled=True)  58.4 us
    all_gather x1, blocking collectives, local(): stats = combine(lax.all_gather(stats, 'vocab', axis=0))  48.6 us
    all_gather x1, waiting for transfers between devices, local(): errors = lax.all_gather(errors, 'fsdp', axis=0, tiled=True)  32.4 us
    all_gather x1, blocking collectives, local(): wanted = lax.all_gather(labels, 'fsdp', axis=0, tiled=True)  22.4 us
    all_gather x1, blocking collectives, local(): states = lax.all_gather(hidden_states.T, 'fsdp', axis=1, tiled=True)  13.1 us
    all_gather x1, blocking collectives, local(): stats = combine(lax.all_gather(stats, 'fsdp', axis=0))  12.8 us
  transfers between devices with their start and end apart: 5, of which 3 were waited for; matrix products, arithmetic and copies ran while one was open for 2% of the time, Pallas kernels for 0%

profile of v1, /device:TPU:26, one launch (start us, length us, event | category | flops | bytes accessed | tf_op | source)
XLA Modules:
  0.0 453.9 jit_solution(14088944663823949947)
XLA Ops:
  7.2 0.0 all-gather.8.cloned.1.call-start
  7.2 13.1 %all_gather.24 = bf16[96,1024]{1,0:T(8,128)(2,1)} all-gather(bf16[96,128]{1,0:T(8,128)(2,1)} %bitcast.67), channel_id=1, replica_groups=mesh['fsdp'=8,'vocab'=32] {'fsdp'}, dimensions={1}, use_global_device_ids=true | all-gather | bytes 221184 | tf_op jit(solution)/shard_map/all_gather | solution.py:20
  20.3 0.0 all-gather.8.cloned.1.call-update
  20.3 2.6 copy.18
  22.9 4.5 all-to-all-start
  27.4 22.4 %all-gather.2 = s32[8,1,128]{2,1,0:T(1,128)S(1)} all-gather(s32[1,1,128]{2,1,0:T(1,128)S(1)} %bitcast.73), channel_id=1, replica_groups=mesh['fsdp'=8,'vocab'=32] {'fsdp'}, dimensions={0}, use_global_device_ids=true | all-gather | bytes 4608 | tf_op jit(solution)/shard_map/all_gather | solution.py:22
  49.8 0.0 all-to-all-done
  49.8 0.7 copy.19
  50.6 58.4 %all-gather.8.cloned.1.call-done = bf16[3072,1024]{1,0:T(8,128)(2,1)} async-done(((bf16[96,1024]{1,0:T(8,128)(2,1)}), bf16[3072,1024]{1,0:T(8,128)(2,1)}) %all-gather.8.cloned.1.call-update) | async-done | bytes 6291472 | tf_op jit(solution)/shard_map/all_gather | solution.py:21
  108.9 4.6 %fusion.15 = (f32[1024]{0:T(1024)S(1)}, f32[256,1024]{1,0:T(8,128)S(1)}) fusion(bf16[3072,256]{1,0:T(8,128)(2,1)S(1)} %bitcast.58, bf16[3072,1024]{1,0:T(8,128)(2,1)} %all-gather.8.cloned.1.call-done), kind=kOutput, calls=%fused_computation.32 | convolution fusion | flops 1610873856 | bytes 8916992 | tf_op jit(solution)/shard_map/dot_general | solution.py:24
  113.5 0.3 exponential_reduce_fusion
  113.8 12.8 %all-gather.3 = f32[8,3,1024]{2,1,0:T(4,128)S(1)} all-gather(f32[1,3,1024]{2,1,0:T(4,128)S(1)} %maximum_bitcast_fusion), channel_id=2, replica_groups=mesh['fsdp'=8,'vocab'=32] {'fsdp'}, dimensions={0}, use_global_device_ids=true | all-gather | bytes 110592 | tf_op jit(solution)/shard_map/all_gather | solution.py:31
  126.6 0.1 fusion.14
  126.7 48.6 %all-gather.4 = f32[32,3,1024]{2,1,0:T(4,128)S(1)} all-gather(f32[1,3,1024]{2,1,0:T(4,128)S(1)} %maximum_bitcast_fusion.1), channel_id=3, replica_groups=mesh['fsdp'=8,'vocab'=32] {'vocab'}, dimensions={0}, use_global_device_ids=true | all-gather | bytes 405504 | tf_op jit(solution)/shard_map/all_gather | solution.py:32
  175.3 0.3 fusion.13
  175.6 0.1 fusion.6
  175.7 1.1 fusion.2
  176.8 0.0 all-gather.10.cloned.1.call-update
  176.8 0.0 reduce-scatter.2.cloned.1.call-start
  176.8 32.4 %all-gather.10.cloned.1.call-done = bf16[2048,1024]{1,0:T(8,128)(2,1)} async-done(((bf16[256,1024]{1,0:T(8,128)(2,1)}), bf16[2048,1024]{1,0:T(8,128)(2,1)}) %all-gather.10.cloned.1.call-update) | async-done | bytes 4194320 | tf_op jit(solution)/shard_map/all_gather | solution.py:37
  209.2 4.6 %convolution_bitcast_fusion = f32[384,1024]{0,1:T(8,128)S(1)} fusion(bf16[2048,1024]{1,0:T(8,128)(2,1)} %all-gather.10.cloned.1.call-done, bf16[384,2048]{1,0:T(8,128)(2,1)S(1)} %copy-done), kind=kOutput, calls=%fused_computation.1 | convolution fusion | flops 1610612736 | bytes 7340032 | tf_op jit(solution)/shard_map/dot_general | solution.py:38
  213.8 0.5 copy.22
  214.3 0.3 copy.29
  214.6 0.1 bitcast_bitcast_fusion
  214.7 1.4 copy.23
  216.2 0.0 reduce-scatter.2.cloned.1.call-update
  216.2 0.6 dynamic_slice.6
  216.8 218.4 %reduce-scatter.2.cloned.1.call-done = f32[1,96,128]{2,1,0:T(8,128)} async-done(((f32[32,96,128]{2,1,0:T(8,128)}), f32[1,96,128]{2,1,0:T(8,128)}) %reduce-scatter.2.cloned.1.call-update) | async-done | bytes 49168 | tf_op jit(solution)/shard_map/reduce_scatter | solution.py:42
  435.2 0.8 convert_bitcast_fusion
  436.0 4.8 %collective-permute-start = (bf16[96,128]{1,0:T(8,128)(2,1)S(1)}, bf16[96,128]{1,0:T(8,128)(2,1)S(1)}, u32[]{:S(2)}, u32[]{:S(2)}) collective-permute-start(bf16[96,128]{1,0:T(8,128)(2,1)S(1)} %convert_bitcast_fusion), channel_id=1, source_target_pairs={{0,0},{1,1},{2,2},{3,3},{4,32},{5,33},{6,34},{7,35},{8,64},{9,65},... | collective-permute-start | bytes 73736 | tf_op jit(solution)/shard_map/ppermute | solution.py:48
  440.8 5.9 %fusion.3 = f32[384,2048]{1,0:T(8,128)} fusion(bf16[2048,1024]{1,0:T(8,128)(2,1)} %all-gather.10.cloned.1.call-done, bf16[3072,1024]{1,0:T(8,128)(2,1)} %all-gather.8.cloned.1.call-done, s32[]{:T(128)S(6)} %select_n.12), kind=kOutput, calls=%fused_computation.8 | convolution fusion | flops 1610612736 | bytes 8126468 | tf_op jit(solution)/shard_map/dot_general | solution.py:50
  446.7 0.6 copy.47
  (11 shorter events, 0.1 us)
Async XLA Ops:
  7.2 101.8 %all-gather.8.cloned.1.call-start = ((), (), s32[]{:S(2)}) async-start(), calls=%async_computation.2 | async-start | bytes 6488064 | tf_op jit(solution)/shard_map/all_gather | solution.py:21
  22.9 4.5 copy-start.1
  22.9 26.9 %all-to-all-start = ((bf16[384,8,256]{0,2,1:T(8,128)(2,1)}), bf16[384,8,256]{0,2,1:T(8,128)(2,1)S(1)}, u32[]{:S(2)}, u32[]{:S(2)}) async-start(bf16[384,8,256]{0,2,1:T(8,128)(2,1)} %bitcast), calls=%async_computation | async-start | bytes 3145728 | tf_op jit(solution)/shard_map/all_to_all | solution.py:23
  27.4 181.8 %all-gather.10.cloned.1.call-start = ((), (), s32[]{:S(2)}) async-start(), calls=%async_computation.3 | async-start | bytes 4718592 | tf_op jit(solution)/shard_map/all_gather | solution.py:37
  175.3 33.9 %copy-start = (bf16[384,2048]{1,0:T(8,128)(2,1)S(1)}, bf16[384,2048]{1,0:T(8,128)(2,1)}, u32[]{:S(2)}) copy-start(bf16[384,2048]{1,0:T(8,128)(2,1)} %param.4) | copy-start | bytes 4718596
  176.8 258.4 %reduce-scatter.2.cloned.1.call-start = ((), (), s32[]{:S(2)}) async-start(), calls=%async_computation.4 | async-start | bytes 1622016 | tf_op jit(solution)/shard_map/reduce_scatter | solution.py:42
  436.0 10.8 %collective-permute-start = (bf16[96,128]{1,0:T(8,128)(2,1)S(1)}, bf16[96,128]{1,0:T(8,128)(2,1)S(1)}, u32[]{:S(2)}, u32[]{:S(2)}) collective-permute-start(bf16[96,128]{1,0:T(8,128)(2,1)S(1)} %convert_bitcast_fusion), channel_id=1, source_target_pairs={{0,0},{1,1},{2,2},{3,3},{4,32},{5,33},{6,34},{7,35},{8,64},{9,65},... | collective-permute-start | bytes 73736 | tf_op jit(solution)/shard_map/ppermute | solution.py:48
Sparse Core Ops, SparseCore 0:
  20.5 88.4 all-gather.7
  176.9 32.2 all-gather.9
  216.3 218.8 reduce-scatter.1

commit v2 on v1

v2 whole, which is shorter than its diff:
```python
import functools

import jax
import jax.numpy as jnp
from jax import lax
from jax.experimental import pallas as pl
from jax.experimental.pallas import tpu as pltpu
from jax.sharding import PartitionSpec as P

X, Y, Z = 4, 4, 8
F32, BF16 = jnp.float32, jnp.bfloat16


def kernel(hid, head, labels, loss_out, state_out, grad_out,
           w, wl, relay, wt, h, hpad, lab, e, errs, hs, gv,
           stx, sty, stz, full, sb, ry, zs, rz, fs, fin, spad,
           load_s, w_s, wl_r, rel_r, w2_r, b1_s, b1_r, lab_s, lab_r,
           hz_s, hz_r, hy_s, hy_r, hd_s, hd_r, e_s, e_r, eh_r,
           sx_s, sx_r, sy_s, sy_r, sz_s, sz_r,
           ry_s, ry_r, rz_s, rz_r, f_s, f_r, g_s):
    f, v = lax.axis_index("fsdp"), lax.axis_index("vocab")
    x, c = lax.div(f, 2), lax.rem(f, 2)
    y, z = lax.div(v, Z), lax.rem(v, Z)
    xp, xm, xo = lax.rem(x + 1, X), lax.rem(x + 3, X), lax.rem(x + 2, X)
    yp, ym, yo = lax.rem(y + 1, Y), lax.rem(y + 3, Y), lax.rem(y + 2, Y)
    fp, fm, fo, fq = 2 * xp + c, 2 * xm + c, 2 * xo + c, 2 * x + 1 - c
    sends = []

    def at_f(g):
        return {"fsdp": g, "vocab": v}

    def at_yz(a, b):
        return {"fsdp": f, "vocab": Z * a + b}

    def send(src, dst, ssem, rsem, device):
        copy = pltpu.make_async_remote_copy(
            src_ref=src, dst_ref=dst, send_sem=ssem, recv_sem=rsem,
            device_id=device, device_id_type=pl.DeviceIdType.MESH)
        copy.start()
        sends.append(copy)

    def arrived(dst, rsem):
        pltpu.make_async_remote_copy(
            src_ref=dst, dst_ref=dst, send_sem=g_s.at[0], recv_sem=rsem,
            device_id=at_f(fq), device_id_type=pl.DeviceIdType.MESH).wait_recv()

    def home(t):
        return {"fsdp": 2 * t + lax.div(z, 4), "vocab": Z * x + 4 * c + y}

    def origin(r):
        return {"fsdp": 2 * y + lax.div(z, 4), "vocab": Z * lax.rem(z, 4) + 4 * c + r}

    own_home = jnp.logical_and(y == x, z == 4 * c + y)

    load_w = pltpu.make_async_copy(head, w, load_s.at[0])
    load_w.start()
    columns = pl.ds(pl.multiple_of(256 * f, 256), 256)
    load_own = pltpu.make_async_copy(head.at[:, columns], wl.at[f], load_s.at[1])
    load_own.start()

    barrier = pltpu.get_barrier_semaphore()

    def hello(device):
        pl.semaphore_signal(barrier, inc=1, device_id=device, device_id_type=pl.DeviceIdType.MESH)

    for k in range(1, 8):
        hello(at_f(lax.rem(f + k, 8)))
    for k in range(1, Y):
        hello(at_yz(lax.rem(y + k, Y), z))
    for k in range(1, Z):
        hello(at_yz(y, lax.rem(z + k, Z)))
    for r in range(4):
        if True:
            @pl.when(jnp.logical_not(jnp.logical_and(own_home, y == r)))
            def _():
                hello(origin(r))

    hpad[...] = jnp.zeros_like(hpad)
    hpad[:, 0:96] = hid[...].astype(F32)
    h[x, c, y, z] = hpad[...].T[0:96].astype(BF16)
    lab[f] = jnp.broadcast_to(labels[...], (8, 128))

    load_w.wait()
    pl.semaphore_wait(barrier, 7 + 3 + 7 + 4 - own_home.astype(jnp.int32))

    mine = h.at[x, c, y, z]
    for i, g in enumerate((fp, fm, fo)):
        send(mine, mine, b1_s.at[i], b1_r.at[x], at_f(g))
    for k in range(1, 8):
        send(lab.at[f], lab.at[f], lab_s.at[k], lab_r.at[f], at_f(lax.rem(f + k, 8)))

    def cols(g):
        return pl.ds(pl.multiple_of(256 * g, 256), 256)

    for d in range(2):
        send(w.at[0:192, cols(2 * xo + d)], relay.at[0, d], w_s.at[d], rel_r.at[0, d], at_f(fp))
        send(w.at[192:384, cols(2 * xo + d)], relay.at[1, d], w_s.at[2 + d], rel_r.at[1, d], at_f(fm))
    send(w.at[:, cols(fq)], wl.at[f], w_s.at[4], wl_r.at[f], at_f(fq))
    for d in range(2):
        send(w.at[:, cols(2 * xp + d)], wl.at[f], w_s.at[5 + d], wl_r.at[f], at_f(2 * xp + d))
        send(w.at[:, cols(2 * xm + d)], wl.at[f], w_s.at[7 + d], wl_r.at[f], at_f(2 * xm + d))

    def hidden_z(t):
        block = h.at[t, c, y, z]

        @pl.when(x != t)
        def _():
            arrived(block, b1_r.at[t])

        for k in range(1, Z):
            send(block, block, hz_s.at[t, k], hz_r.at[t, k], at_yz(y, lax.rem(z + k, Z)))

    for t in range(X):
        hidden_z(t)

    for d in range(2):
        arrived(relay.at[0, d], rel_r.at[0, d])
        send(relay.at[0, d], wl.at[fm, 0:192], w_s.at[9 + d], w2_r.at[0, c], at_f(2 * xp + d))
        arrived(relay.at[1, d], rel_r.at[1, d])
        send(relay.at[1, d], wl.at[fp, 192:384], w_s.at[11 + d], w2_r.at[1, c], at_f(2 * xm + d))

    def to_partner(t, row, n):
        block = h.at[t, c, row]
        send(block, block, hd_s.at[t, n], hd_r.at[t, n], at_f(fq))

    def hidden_y(t):
        for k in range(1, Z):
            arrived(h.at[t, c, y, lax.rem(z + Z - k, Z)], hz_r.at[t, k])
        block = h.at[t, c, y]
        send(block, block, hy_s.at[t, 0], hy_r.at[t, 0], at_yz(yp, z))
        send(block, block, hy_s.at[t, 1], hy_r.at[t, 1], at_yz(ym, z))
        to_partner(t, y, 0)

    def hidden_y2(t):
        arrived(h.at[t, c, ym], hy_r.at[t, 0])
        block = h.at[t, c, ym, 0:4]
        send(block, block, hy_s.at[t, 2], hy_r.at[t, 2], at_yz(yp, z))
        arrived(h.at[t, c, yp], hy_r.at[t, 1])
        block = h.at[t, c, yp, 4:8]
        send(block, block, hy_s.at[t, 3], hy_r.at[t, 3], at_yz(ym, z))
        to_partner(t, ym, 1)
        to_partner(t, yp, 2)

    def hidden_end(t):
        arrived(h.at[t, c, yo, 0:4], hy_r.at[t, 2])
        arrived(h.at[t, c, yo, 4:8], hy_r.at[t, 3])
        to_partner(t, yo, 3)

    def hidden_all(t):
        for n, row in enumerate((y, ym, yp, yo)):
            arrived(h.at[t, 1 - c, row], hd_r.at[t, n])

    hidden_y(0)
    hidden_y(1)
    hidden_y2(0)
    hidden_y(2)
    hidden_end(0)
    hidden_y2(1)

    load_own.wait()
    for g in (fq, 2 * xp, 2 * xp + 1, 2 * xm, 2 * xm + 1):
        arrived(wl.at[g], wl_r.at[g])
    for d in range(2):
        arrived(wl.at[2 * xo + d, 0:192], w2_r.at[0, d])
        arrived(wl.at[2 * xo + d, 192:384], w2_r.at[1, d])
    for g in range(8):
        wt[:, 384 * g:384 * g + 384] = wl[g].T
    for k in range(1, 8):
        g = lax.rem(f + k, 8)
        arrived(lab.at[g], lab_r.at[g])

    def wanted(t):
        return jnp.concatenate([lab[2 * t, 0:1, :], lab[2 * t + 1, 0:1, :]], axis=1)

    def rows_of(g):
        return v * 2048 + g * 256 + lax.broadcasted_iota(jnp.int32, (256, 256), 0)

    def forward(t):
        hidden_all(t)
        states = jnp.concatenate(
            [h[t, 0].reshape(3072, 128), h[t, 1].reshape(3072, 128)], axis=1)
        logits = jnp.dot(wt[...], states, preferred_element_type=F32)
        peak = jnp.max(logits, axis=0, keepdims=True)
        shifted = jnp.exp(logits - peak)
        hits = rows_of(f) == wanted(t)
        stx[t, f, 0:1, :] = peak
        stx[t, f, 1:2, :] = jnp.sum(shifted, axis=0, keepdims=True)
        stx[t, f, 2:3, :] = jnp.sum(jnp.where(hits, logits, 0.0), axis=0, keepdims=True)
        e[t, f] = shifted.astype(BF16)
        for k in range(1, 8):
            g = lax.rem(f + k, 8)
            send(stx.at[t, f], stx.at[t, f], sx_s.at[t, k], sx_r.at[t, f], at_f(g))
        block = e.at[t, f]
        send(block, block, e_s.at[t, 0], e_r.at[t, f], at_f(fp))
        send(block, block, e_s.at[t, 1], e_r.at[t, f], at_f(fm))
        send(block, block, e_s.at[t, 2], e_r.at[t, f], at_f(fq))

    def errors_2(t):
        arrived(e.at[t, fm], e_r.at[t, fm])
        block = e.at[t, fm, 0:128]
        send(block, block, e_s.at[t, 3], eh_r.at[t, 0], at_f(fp))
        arrived(e.at[t, fp], e_r.at[t, fp])
        block = e.at[t, fp, 128:256]
        send(block, block, e_s.at[t, 4], eh_r.at[t, 1], at_f(fm))
        for i, g in enumerate((fm, fp)):
            send(e.at[t, g], e.at[t, g], e_s.at[t, 5 + i], e_r.at[t, g], at_f(fq))

    def errors_3(t):
        arrived(e.at[t, fo, 0:128], eh_r.at[t, 0])
        arrived(e.at[t, fo, 128:256], eh_r.at[t, 1])
        send(e.at[t, fo], e.at[t, fo], e_s.at[t, 7], e_r.at[t, fo], at_f(fq))

    def combine(ref, t, n):
        peaks = [ref[t, i, 0:1, :] for i in range(n)]
        peak = functools.reduce(jnp.maximum, peaks)
        total = sum(ref[t, i, 1:2, :] * jnp.exp(peaks[i] - peak) for i in range(n))
        target = sum(ref[t, i, 2:3, :] for i in range(n))
        return peak, total, target

    def put(ref, t, i, values):
        for row, value in enumerate(values):
            ref[t, i, row:row + 1, :] = value

    def stats_y(t):
        for k in range(1, 8):
            g = lax.rem(f + k, 8)
            arrived(stx.at[t, g], sx_r.at[t, g])
        put(sty, t, y, combine(stx, t, 8))
        for k in range(1, Y):
            send(sty.at[t, y], sty.at[t, y], sy_s.at[t, k], sy_r.at[t, k], at_yz(lax.rem(y + k, Y), z))

    def stats_z(t):
        for k in range(1, Y):
            arrived(sty.at[t, lax.rem(y + Y - k, Y)], sy_r.at[t, k])
        put(stz, t, z, combine(sty, t, Y))
        for k in range(1, Z):
            send(stz.at[t, z], stz.at[t, z], sz_s.at[t, k], sz_r.at[t, k], at_yz(y, lax.rem(z + k, Z)))

    def backward(t):
        for k in range(1, Z):
            arrived(stz.at[t, lax.rem(z + Z - k, Z)], sz_r.at[t, k])
        peak, total, target = combine(stz, t, Z)
        full[t, 0:1, :] = jnp.log(total) + peak - target
        at_label = jnp.exp(target - peak) / total - 1.0
        for a in range(X):
            g = 2 * a + 1 - c
            arrived(e.at[t, g], e_r.at[t, g])
        for g in range(8):
            scale = jnp.exp(stx[t, g, 0:1, :] - peak) / total
            value = e[t, g].astype(F32) * scale
            value = jnp.where(rows_of(g) == wanted(t), at_label, value)
            errs[g, :, 256 * t:256 * t + 256] = value.astype(BF16)
        terms = jnp.dot(w[...], errs[:, :, 256 * t:256 * t + 256].reshape(2048, 256),
                        preferred_element_type=F32)
        sb[t] = terms.reshape(4, 96, 256)
        for k in range(1, Y):
            a = lax.rem(y + k, Y)
            send(sb.at[t, a], ry.at[t, k - 1], ry_s.at[t, k - 1], ry_r.at[t, k - 1], at_yz(a, z))

    def reduce_y(t):
        total = sb[t, y]
        for k in range(Y - 1):
            arrived(ry.at[t, k], ry_r.at[t, k])
            total = total + ry[t, k]
        for d in range(2):
            for r in range(4):
                zs[t, 4 * d + r] = total[24 * r:24 * r + 24, 128 * d:128 * d + 128]
        for k in range(1, Z):
            b = lax.rem(z + k, Z)
            send(zs.at[t, b], rz.at[t, k - 1], rz_s.at[t, k - 1], rz_r.at[t, k - 1], at_yz(y, b))

    def home_copy(t):
        return pltpu.make_async_remote_copy(
            src_ref=fs.at[t], dst_ref=fin.at[lax.rem(z, 4)], send_sem=f_s.at[t], recv_sem=f_r.at[lax.rem(z, 4)],
            device_id=home(t), device_id_type=pl.DeviceIdType.MESH)

    def reduce_z(t):
        total = zs[t, z]
        for k in range(Z - 1):
            arrived(rz.at[t, k], rz_r.at[t, k])
            total = total + rz[t, k]
        fs[t] = total
        stays = jnp.logical_and(own_home, x == t)

        @pl.when(stays)
        def _():
            fin[lax.rem(z, 4)] = fs[t]

        @pl.when(jnp.logical_not(stays))
        def _():
            home_copy(t).start()

    forward(0)
    hidden_y(3)
    hidden_end(1)
    forward(1)
    stats_y(0)
    errors_2(0)
    hidden_y2(2)
    hidden_end(2)
    forward(2)
    stats_y(1)
    stats_z(0)
    errors_2(1)
    errors_3(0)
    hidden_y2(3)
    hidden_end(3)
    forward(3)
    stats_y(2)
    stats_z(1)
    errors_2(2)
    errors_3(1)
    backward(0)
    stats_y(3)
    stats_z(2)
    errors_2(3)
    errors_3(2)
    backward(1)
    reduce_y(0)
    stats_z(3)
    errors_3(3)
    backward(2)
    reduce_y(1)
    reduce_z(0)
    backward(3)

    for t in range(X):
        for d in range(2):
            hs[:, 256 * t + 128 * d:256 * t + 128 * d + 128] = h[t, d, x, pl.ds(4 * c, 4)].reshape(384, 128)
    writes = []
    for g in range(8):
        gv[g] = lax.dot_general(hs[...], errs[g], (((1,), (1,)), ((), ())), preferred_element_type=F32)
        write = pltpu.make_async_copy(gv.at[g], grad_out.at[:, 256 * g:256 * g + 256], g_s.at[1 + g])
        write.start()
        writes.append(write)
        if g == 1:
            reduce_y(2)
        if g == 3:
            reduce_z(1)
    reduce_y(3)
    reduce_z(2)
    losses = full[x, 0:1, :]
    loss_out[...] = jnp.where(c == 0, losses[:, 0:128], losses[:, 128:256])
    reduce_z(3)
    for r in range(4):
        @pl.when(jnp.logical_not(jnp.logical_and(own_home, y == r)))
        def _():
            arrived(fin.at[r], f_r.at[r])
    spad[...] = jnp.zeros_like(spad)
    for r in range(4):
        spad[24 * r:24 * r + 24, :] = fin[r]
    state_out[...] = spad[...].T[:, 0:96].astype(BF16)
    for copy in sends:
        copy.wait_send()
    for t in range(X):
        @pl.when(jnp.logical_not(jnp.logical_and(own_home, x == t)))
        def _():
            home_copy(t).wait_send()
    for write in writes:
        write.wait()


def local(hidden_states, head, labels):
    dma = pltpu.SemaphoreType.DMA
    vmem = pltpu.VMEM
    loss, state, grad = pl.pallas_call(
        kernel,
        name="head_loss",
        out_shape=(
            jax.ShapeDtypeStruct((1, 128), F32),
            jax.ShapeDtypeStruct((128, 96), BF16),
            jax.ShapeDtypeStruct((384, 2048), F32),
        ),
        in_specs=[
            pl.BlockSpec(memory_space=vmem),
            pl.BlockSpec(memory_space=pl.ANY),
            pl.BlockSpec(memory_space=vmem),
        ],
        out_specs=(
            pl.BlockSpec(memory_space=vmem),
            pl.BlockSpec(memory_space=vmem),
            pl.BlockSpec(memory_space=pl.ANY),
        ),
        scratch_shapes=[
            vmem((384, 2048), BF16),
            vmem((8, 384, 256), BF16),
            vmem((2, 2, 192, 256), BF16),
            vmem((256, 3072), BF16),
            vmem((X, 2, Y, Z, 96, 128), BF16),
            vmem((128, 128), F32),
            vmem((8, 8, 128), jnp.int32),
            vmem((X, 8, 256, 256), BF16),
            vmem((8, 256, 1024), BF16),
            vmem((384, 1024), BF16),
            vmem((8, 384, 256), F32),
            vmem((X, 8, 8, 256), F32),
            vmem((X, Y, 8, 256), F32),
            vmem((X, Z, 8, 256), F32),
            vmem((X, 8, 256), F32),
            vmem((X, 4, 96, 256), F32),
            vmem((X, Y - 1, 96, 256), F32),
            vmem((X, Z, 24, 128), F32),
            vmem((X, Z - 1, 24, 128), F32),
            vmem((X, 24, 128), F32),
            vmem((4, 24, 128), F32),
            vmem((128, 128), F32),
            dma((2,)), dma((13,)), dma((8,)), dma((2, 2)), dma((2, 2)),
            dma((3,)), dma((X,)), dma((8,)), dma((8,)),
            dma((X, Z)), dma((X, Z)), dma((X, 4)), dma((X, 4)), dma((X, 4)), dma((X, 4)),
            dma((X, 8)), dma((X, 8)), dma((X, 2)),
            dma((X, 8)), dma((X, 8)), dma((X, Y)), dma((X, Y)), dma((X, Z)), dma((X, Z)),
            dma((X, Y - 1)), dma((X, Y - 1)), dma((X, Z - 1)), dma((X, Z - 1)),
            dma((X,)), dma((4,)), dma((9,)),
        ],
        compiler_params=pltpu.CompilerParams(
            collective_id=0, has_side_effects=True, vmem_limit_bytes=60 * 1024 * 1024),
    )(hidden_states, head, labels.reshape(1, 128))
    return (loss.reshape(128), state, grad)


def solution(mesh):
    in_specs = (P("fsdp", "vocab"), P("fsdp", "vocab"), P("fsdp"))
    out_specs = (P("fsdp"), P("fsdp", "vocab"), P("fsdp", "vocab"))
    return jax.shard_map(local, mesh=mesh, in_specs=in_specs, out_specs=out_specs, check_vma=False)
```

time: 459 us -> 107 us (0.23)
  the two profiles are of different devices: /device:TPU:26 before, /device:TPU:7 now
where the time goes in v2:
time: 107 us
  Pallas kernels  98.2 us (92%)
  local copies, waits for them, and re-layouts  7.94 us (7%)
    pallas_call x1, Pallas kernels, local(): pl.pallas_call(kernel, name='head_loss', out_shape=(jax.ShapeDtypeStruct(...  98.2 us
    unnamed x4, local copies, waits for them, and re-layouts  7.94 us

profile of v2, /device:TPU:7, one launch (start us, length us, event | category | flops | bytes accessed | tf_op | source)
XLA Modules:
  0.0 106.8 jit_solution(15513065340824772898)
XLA Ops:
  0.6 1.5 %copy.6.hid = bf16[128,96]{1,0:T(8,128)(2,1)} copy(bf16[128,96]{0,1:T(8,128)(2,1)} %param.3) | data formatting | bytes 49152 | tf_op args[0]
  2.1 98.2 %head_loss.1 = (f32[1,128]{1,0:T(1,128)}, bf16[128,96]{1,0:T(8,128)(2,1)}, f32[384,2048]{1,0:T(8,128)}) custom-call(bf16[128,96]{1,0:T(8,128)(2,1)} %copy.6.hid, bf16[384,2048]{1,0:T(8,128)(2,1)} %head.1, s32[1,128]{1,0:T(1,128)} %bitcast.2), custom_call_target="tpu_custom_call" | custom-call | tf_op jit(solution)/shard_map/head_loss/pallas_call | solution.py:366
  100.3 1.5 %copy.7 = bf16[128,96]{0,1:T(8,128)(2,1)} copy(bf16[128,96]{1,0:T(8,128)(2,1)} %get-tuple-element.10) | data formatting | bytes 49152
  101.8 1.1 %copy.10 = f32[128]{0:T(128)} copy(f32[128]{0:T(128)} %bitcast.3) | data formatting | bytes 1024
  102.9 3.9 %copy.11 = f32[384,2048]{1,0:T(8,128)} copy(f32[384,2048]{1,0:T(8,128)} %get-tuple-element.17) | data formatting | bytes 6291456

commit v3 on v2

--- a/solution.py
+++ b/solution.py
@@ -8,14 +8,16 @@
 from jax.sharding import PartitionSpec as P
 
 X, Y, Z = 4, 4, 8
+LIMIT = 44
+R = 2
 F32, BF16 = jnp.float32, jnp.bfloat16
 
 
 def kernel(hid, head, labels, loss_out, state_out, grad_out,
-           w, wl, relay, wt, h, hpad, lab, e, errs, hs, gv,
-           stx, sty, stz, full, sb, ry, zs, rz, fs, fin, spad,
+           w, wl, relay, wt, h, lab, e, errs, hs,
+           stx, sty, stz, full, sb, ry, zs, rz, fs, fin,
            load_s, w_s, wl_r, rel_r, w2_r, b1_s, b1_r, lab_s, lab_r,
-           hz_s, hz_r, hy_s, hy_r, hd_s, hd_r, e_s, e_r, eh_r,
+           hz_s, hz_r, hy_s, hy_r, hd_s, hd_r, hr_s, hr_r, rd_s, rd_r, e_s, e_r, eh_r,
            sx_s, sx_r, sy_s, sy_r, sz_s, sz_r,
            ry_s, ry_r, rz_s, rz_r, f_s, f_r, g_s):
     f, v = lax.axis_index("fsdp"), lax.axis_index("vocab")
@@ -70,18 +72,22 @@
     for k in range(1, Z):
         hello(at_yz(y, lax.rem(z + k, Z)))
     for r in range(4):
-        if True:
-            @pl.when(jnp.logical_not(jnp.logical_and(own_home, y == r)))
-            def _():
-                hello(origin(r))
-
-    hpad[...] = jnp.zeros_like(hpad)
-    hpad[:, 0:96] = hid[...].astype(F32)
-    h[x, c, y, z] = hpad[...].T[0:96].astype(BF16)
-    lab[f] = jnp.broadcast_to(labels[...], (8, 128))
-
-    load_w.wait()
-    pl.semaphore_wait(barrier, 7 + 3 + 7 + 4 - own_home.astype(jnp.int32))
+        @pl.when(jnp.logical_not(jnp.logical_and(own_home, y == r)))
+        def _():
+            hello(origin(r))
+
+    load_hid = pltpu.make_async_copy(hid, h.at[x, c, y, z], load_s.at[2])
+    load_hid.start()
+    load_lab = pltpu.make_async_copy(labels, lab.at[f, 0:1], load_s.at[3])
+    load_lab.start()
+
+    def begin():
+        load_w.wait()
+        load_hid.wait()
+        load_lab.wait()
+        pl.semaphore_wait(barrier, 7 + 3 + 7 + 4 - own_home.astype(jnp.int32))
+
+    begin()
 
     mine = h.at[x, c, y, z]
     for i, g in enumerate((fp, fm, fo)):
@@ -110,14 +116,59 @@
         for k in range(1, Z):
             send(block, block, hz_s.at[t, k], hz_r.at[t, k], at_yz(y, lax.rem(z + k, Z)))
 
-    for t in range(X):
-        hidden_z(t)
-
-    for d in range(2):
-        arrived(relay.at[0, d], rel_r.at[0, d])
-        send(relay.at[0, d], wl.at[fm, 0:192], w_s.at[9 + d], w2_r.at[0, c], at_f(2 * xp + d))
-        arrived(relay.at[1, d], rel_r.at[1, d])
-        send(relay.at[1, d], wl.at[fp, 192:384], w_s.at[11 + d], w2_r.at[1, c], at_f(2 * xm + d))
+    def ring_y():
+        block = h.at[R, c, y, z]
+
+        @pl.when(x != R)
+        def _():
+            arrived(block, b1_r.at[R])
+
+        for k in range(1, Y):
+            send(block, block, hz_s.at[R, k], hz_r.at[R, k], at_yz(lax.rem(y + k, Y), z))
+
+    zp, zm = lax.rem(z + 1, Z), lax.rem(z + Z - 1, Z)
+
+    def ring_send(step):
+        right = lax.rem(z + Z + 1 - step, Z)
+        left = lax.rem(z + step - 1, Z)
+        low, high = ((0, 4), (0, 4)) if step < 4 else ((0, 2), (2, 4))
+        block = h.at[R, c, low[0]:low[1], right]
+        send(block, block, hr_s.at[0, step], hr_r.at[0, step], at_yz(y, zp))
+        block = h.at[R, c, high[0]:high[1], left]
+        send(block, block, hr_s.at[1, step], hr_r.at[1, step], at_yz(y, zm))
+
+    def ring_partner(n, column):
+        block = h.at[R, c, :, column]
+        send(block, block, rd_s.at[n], rd_r.at[n], at_f(fq))
+
+    def ring_start():
+        for k in range(1, Y):
+            arrived(h.at[R, c, lax.rem(y + Y - k, Y), z], hz_r.at[R, k])
+        ring_send(1)
+        ring_partner(0, z)
+
+    def ring_next(step):
+        left, right = lax.rem(z + Z - step, Z), lax.rem(z + step, Z)
+        arrived(h.at[R, c, :, left], hr_r.at[0, step])
+        arrived(h.at[R, c, :, right], hr_r.at[1, step])
+        ring_send(step + 1)
+        ring_partner(2 * step - 1, left)
+        ring_partner(2 * step, right)
+
+    def ring_end():
+        far = lax.rem(z + 4, Z)
+        arrived(h.at[R, c, 0:2, far], hr_r.at[0, 4])
+        arrived(h.at[R, c, 2:4, far], hr_r.at[1, 4])
+        ring_partner(7, far)
+
+
+    def relays():
+        for d in range(2):
+            arrived(relay.at[0, d], rel_r.at[0, d])
+            send(relay.at[0, d], wl.at[fm, 0:192], w_s.at[9 + d], w2_r.at[0, c], at_f(2 * xp + d))
+            arrived(relay.at[1, d], rel_r.at[1, d])
+            send(relay.at[1, d], wl.at[fp, 192:384], w_s.at[11 + d], w2_r.at[1, c], at_f(2 * xm + d))
+
 
     def to_partner(t, row, n):
         block = h.at[t, c, row]
@@ -126,43 +177,57 @@
     def hidden_y(t):
         for k in range(1, Z):
             arrived(h.at[t, c, y, lax.rem(z + Z - k, Z)], hz_r.at[t, k])
-        block = h.at[t, c, y]
-        send(block, block, hy_s.at[t, 0], hy_r.at[t, 0], at_yz(yp, z))
-        send(block, block, hy_s.at[t, 1], hy_r.at[t, 1], at_yz(ym, z))
+        low, high = h.at[t, c, y, 0:4], h.at[t, c, y, 4:8]
+        send(low, low, hy_s.at[t, 0], hy_r.at[t, 0], at_yz(yp, z))
+        send(high, high, hy_s.at[t, 1], hy_r.at[t, 1], at_yz(ym, z))
+        send(high, high, hy_s.at[t, 4], hy_r.at[t, 4], at_yz(yp, z))
+        send(low, low, hy_s.at[t, 5], hy_r.at[t, 5], at_yz(ym, z))
         to_partner(t, y, 0)
 
     def hidden_y2(t):
-        arrived(h.at[t, c, ym], hy_r.at[t, 0])
         block = h.at[t, c, ym, 0:4]
+        arrived(block, hy_r.at[t, 0])
         send(block, block, hy_s.at[t, 2], hy_r.at[t, 2], at_yz(yp, z))
-        arrived(h.at[t, c, yp], hy_r.at[t, 1])
         block = h.at[t, c, yp, 4:8]
+        arrived(block, hy_r.at[t, 1])
         send(block, block, hy_s.at[t, 3], hy_r.at[t, 3], at_yz(ym, z))
+
+    def hidden_end(t):
+        arrived(h.at[t, c, ym, 4:8], hy_r.at[t, 4])
+        arrived(h.at[t, c, yp, 0:4], hy_r.at[t, 5])
         to_partner(t, ym, 1)
         to_partner(t, yp, 2)
-
-    def hidden_end(t):
         arrived(h.at[t, c, yo, 0:4], hy_r.at[t, 2])
         arrived(h.at[t, c, yo, 4:8], hy_r.at[t, 3])
         to_partner(t, yo, 3)
 
     def hidden_all(t):
-        for n, row in enumerate((y, ym, yp, yo)):
-            arrived(h.at[t, 1 - c, row], hd_r.at[t, n])
-
+        if t == R:
+            for n, k in enumerate((0, 7, 1, 6, 2, 5, 3, 4)):
+                arrived(h.at[t, 1 - c, :, lax.rem(z + k, Z)], rd_r.at[n])
+        else:
+            for n, row in enumerate((y, ym, yp, yo)):
+                arrived(h.at[t, 1 - c, row], hd_r.at[t, n])
+
+    def head_in():
+        load_own.wait()
+        for g in (fq, 2 * xp, 2 * xp + 1, 2 * xm, 2 * xm + 1):
+            arrived(wl.at[g], wl_r.at[g])
+        for d in range(2):
+            arrived(wl.at[2 * xo + d, 0:192], w2_r.at[0, d])
+            arrived(wl.at[2 * xo + d, 192:384], w2_r.at[1, d])
+
+    hidden_z(0)
+    hidden_z(1)
+    hidden_z(3)
+    ring_y()
+    ring_start()
+    relays()
     hidden_y(0)
+    hidden_y2(0)
     hidden_y(1)
-    hidden_y2(0)
-    hidden_y(2)
-    hidden_end(0)
-    hidden_y2(1)
-
-    load_own.wait()
-    for g in (fq, 2 * xp, 2 * xp + 1, 2 * xm, 2 * xm + 1):
-        arrived(wl.at[g], wl_r.at[g])
-    for d in range(2):
-        arrived(wl.at[2 * xo + d, 0:192], w2_r.at[0, d])
-        arrived(wl.at[2 * xo + d, 192:384], w2_r.at[1, d])
+    ring_next(1)
+    head_in()
     for g in range(8):
         wt[:, 384 * g:384 * g + 384] = wl[g].T
     for k in range(1, 8):
@@ -190,22 +255,26 @@
         for k in range(1, 8):
             g = lax.rem(f + k, 8)
             send(stx.at[t, f], stx.at[t, f], sx_s.at[t, k], sx_r.at[t, f], at_f(g))
-        block = e.at[t, f]
-        send(block, block, e_s.at[t, 0], e_r.at[t, f], at_f(fp))
-        send(block, block, e_s.at[t, 1], e_r.at[t, f], at_f(fm))
+        low, high, block = e.at[t, f, 0:128], e.at[t, f, 128:256], e.at[t, f]
+        send(low, low, e_s.at[t, 0], eh_r.at[t, 2], at_f(fp))
+        send(high, high, e_s.at[t, 1], eh_r.at[t, 3], at_f(fm))
+        send(high, high, e_s.at[t, 8], eh_r.at[t, 4], at_f(fp))
+        send(low, low, e_s.at[t, 9], eh_r.at[t, 5], at_f(fm))
         send(block, block, e_s.at[t, 2], e_r.at[t, f], at_f(fq))
 
     def errors_2(t):
-        arrived(e.at[t, fm], e_r.at[t, fm])
         block = e.at[t, fm, 0:128]
+        arrived(block, eh_r.at[t, 2])
         send(block, block, e_s.at[t, 3], eh_r.at[t, 0], at_f(fp))
-        arrived(e.at[t, fp], e_r.at[t, fp])
         block = e.at[t, fp, 128:256]
+        arrived(block, eh_r.at[t, 3])
         send(block, block, e_s.at[t, 4], eh_r.at[t, 1], at_f(fm))
+
+    def errors_3(t):
+        arrived(e.at[t, fm, 128:256], eh_r.at[t, 4])
+        arrived(e.at[t, fp, 0:128], eh_r.at[t, 5])
         for i, g in enumerate((fm, fp)):
             send(e.at[t, g], e.at[t, g], e_s.at[t, 5 + i], e_r.at[t, g], at_f(fq))
-
-    def errors_3(t):
         arrived(e.at[t, fo, 0:128], eh_r.at[t, 0])
         arrived(e.at[t, fo, 128:256], eh_r.at[t, 1])
         send(e.at[t, fo], e.at[t, fo], e_s.at[t, 7], e_r.at[t, fo], at_f(fq))
@@ -290,49 +359,49 @@
         def _():
             home_copy(t).start()
 
+    hidden_end(0)
     forward(0)
+    hidden_y2(1)
     hidden_y(3)
+    ring_next(2)
     hidden_end(1)
     forward(1)
+    errors_2(0)
+    ring_next(3)
+    hidden_y2(3)
     stats_y(0)
-    errors_2(0)
-    hidden_y2(2)
-    hidden_end(2)
+    ring_end()
     forward(2)
+    errors_2(1)
+    errors_3(0)
     stats_y(1)
     stats_z(0)
-    errors_2(1)
-    errors_3(0)
-    hidden_y2(3)
     hidden_end(3)
     forward(3)
+    errors_2(2)
+    errors_3(1)
     stats_y(2)
     stats_z(1)
-    errors_2(2)
-    errors_3(1)
+    stats_y(3)
     backward(0)
-    stats_y(3)
+    errors_2(3)
     stats_z(2)
-    errors_2(3)
     errors_3(2)
+    stats_z(3)
     backward(1)
-    reduce_y(0)
-    stats_z(3)
     errors_3(3)
     backward(2)
+    reduce_y(0)
+    backward(3)
     reduce_y(1)
     reduce_z(0)
-    backward(3)
 
     for t in range(X):
         for d in range(2):
             hs[:, 256 * t + 128 * d:256 * t + 128 * d + 128] = h[t, d, x, pl.ds(4 * c, 4)].reshape(384, 128)
-    writes = []
     for g in range(8):
-        gv[g] = lax.dot_general(hs[...], errs[g], (((1,), (1,)), ((), ())), preferred_element_type=F32)
-        write = pltpu.make_async_copy(gv.at[g], grad_out.at[:, 256 * g:256 * g + 256], g_s.at[1 + g])
-        write.start()
-        writes.append(write)
+        grad_out[:, 256 * g:256 * g + 256] = lax.dot_general(
+            hs[...], errs[g], (((1,), (1,)), ((), ())), preferred_element_type=F32)
         if g == 1:
             reduce_y(2)
         if g == 3:
@@ -346,18 +415,17 @@
         @pl.when(jnp.logical_not(jnp.logical_and(own_home, y == r)))
         def _():
             arrived(fin.at[r], f_r.at[r])
-    spad[...] = jnp.zeros_like(spad)
-    for r in range(4):
-        spad[24 * r:24 * r + 24, :] = fin[r]
-    state_out[...] = spad[...].T[:, 0:96].astype(BF16)
-    for copy in sends:
-        copy.wait_send()
-    for t in range(X):
-        @pl.when(jnp.logical_not(jnp.logical_and(own_home, x == t)))
-        def _():
-            home_copy(t).wait_send()
-    for write in writes:
-        write.wait()
+    state_out[...] = fin[...].reshape(96, 128).astype(BF16)
+
+    def drain():
+        for copy in sends:
+            copy.wait_send()
+        for t in range(X):
+            @pl.when(jnp.logical_not(jnp.logical_and(own_home, x == t)))
+            def _():
+                home_copy(t).wait_send()
+
+    drain()
 
 
 def local(hidden_states, head, labels):
@@ -368,18 +436,14 @@
         name="head_loss",
         out_shape=(
             jax.ShapeDtypeStruct((1, 128), F32),
-            jax.ShapeDtypeStruct((128, 96), BF16),
+            jax.ShapeDtypeStruct((96, 128), BF16),
             jax.ShapeDtypeStruct((384, 2048), F32),
         ),
-        in_specs=[
-            pl.BlockSpec(memory_space=vmem),
-            pl.BlockSpec(memory_space=pl.ANY),
-            pl.BlockSpec(memory_space=vmem),
-        ],
+        in_specs=[pl.BlockSpec(memory_space=pltpu.HBM)] * 3,
         out_specs=(
             pl.BlockSpec(memory_space=vmem),
             pl.BlockSpec(memory_space=vmem),
-            pl.BlockSpec(memory_space=pl.ANY),
+            pl.BlockSpec(memory_space=vmem),
         ),
         scratch_shapes=[
             vmem((384, 2048), BF16),
@@ -387,12 +451,10 @@
             vmem((2, 2, 192, 256), BF16),
             vmem((256, 3072), BF16),
             vmem((X, 2, Y, Z, 96, 128), BF16),
-            vmem((128, 128), F32),
             vmem((8, 8, 128), jnp.int32),
             vmem((X, 8, 256, 256), BF16),
             vmem((8, 256, 1024), BF16),
             vmem((384, 1024), BF16),
-            vmem((8, 384, 256), F32),
             vmem((X, 8, 8, 256), F32),
             vmem((X, Y, 8, 256), F32),
             vmem((X, Z, 8, 256), F32),
@@ -403,19 +465,20 @@
             vmem((X, Z - 1, 24, 128), F32),
             vmem((X, 24, 128), F32),
             vmem((4, 24, 128), F32),
-            vmem((128, 128), F32),
-            dma((2,)), dma((13,)), dma((8,)), dma((2, 2)), dma((2, 2)),
+            dma((4,)), dma((13,)), dma((8,)), dma((2, 2)), dma((2, 2)),
             dma((3,)), dma((X,)), dma((8,)), dma((8,)),
-            dma((X, Z)), dma((X, Z)), dma((X, 4)), dma((X, 4)), dma((X, 4)), dma((X, 4)),
-            dma((X, 8)), dma((X, 8)), dma((X, 2)),
+            dma((X, Z)), dma((X, Z)), dma((X, 6)), dma((X, 6)), dma((X, 4)), dma((X, 4)),
+            dma((2, 5)), dma((2, 5)), dma((8,)), dma((8,)),
+            dma((X, 10)), dma((X, 8)), dma((X, 6)),
             dma((X, 8)), dma((X, 8)), dma((X, Y)), dma((X, Y)), dma((X, Z)), dma((X, Z)),
             dma((X, Y - 1)), dma((X, Y - 1)), dma((X, Z - 1)), dma((X, Z - 1)),
-            dma((X,)), dma((4,)), dma((9,)),
+            dma((X,)), dma((4,)), dma((1,)),
         ],
         compiler_params=pltpu.CompilerParams(
-            collective_id=0, has_side_effects=True, vmem_limit_bytes=60 * 1024 * 1024),
-    )(hidden_states, head, labels.reshape(1, 128))
-    return (loss.reshape(128), state, grad)
+            collective_id=0, has_side_effects=True, vmem_limit_bytes=LIMIT * 1024 * 1024),
+    )(*(pltpu.with_memory_space_constraint(a, pltpu.HBM)
+        for a in (hidden_states.T, head, labels.reshape(1, 128))))
+    return (loss.reshape(128), state.T, grad)
 
 
 def solution(mesh):

time: 107 us -> 95.6 us (0.89)
  Pallas kernels: 98.2 us -> 92.1 us
  local copies, waits for them, and re-layouts: 7.94 us -> 2.78 us
    pallas_call x1, Pallas kernels: 98.2 us -> 92.1 us  [local(): pl.pallas_call(kernel, name='head_loss', out_shape=(jax.ShapeDtypeStruct(...]
    unnamed x4 -> x3, local copies, waits for them, and re-layouts: 7.94 us -> 2.78 us
where the time goes in v3:
time: 95.6 us; the launch traced here: 95.5 us
  Pallas kernels  92.1 us (96%)
  local copies, waits for them, and re-layouts  2.78 us (3%)
    pallas_call x1, Pallas kernels, local(): pl.pallas_call(kernel, name='head_loss', out_shape=(jax.ShapeDtypeStruct(...  92.1 us
    unnamed x3, local copies, waits for them, and re-layouts  2.78 us

profile of v3, /device:TPU:7, one launch (start us, length us, event | category | flops | bytes accessed | tf_op | source)
XLA Modules:
  0.0 95.5 jit_solution(581999222002295290)
XLA Ops:
  0.6 92.1 %head_loss.1 = (f32[1,128]{1,0:T(1,128)S(1)}, bf16[96,128]{1,0:T(8,128)(2,1)S(1)}, f32[384,2048]{1,0:T(8,128)S(1)}) custom-call(bf16[96,128]{1,0:T(8,128)(2,1)} %bitcast.6, bf16[384,2048]{1,0:T(8,128)(2,1)} %head.1, s32[1,128]{1,0:T(1,128)} %bitcast.7), custom_call_target="tpu_custom_call" | custom-call | tf_op jit(solution)/shard_map/head_loss/pallas_call | solution.py:434
  92.8 0.5 copy.9
  93.3 0.6 copy.10
  93.9 1.7 %copy.11 = f32[384,2048]{1,0:T(8,128)} copy(f32[384,2048]{1,0:T(8,128)S(1)} %get-tuple-element.14) | data formatting | bytes 6291456

commit v4 on v3

v4 whole, which is shorter than its diff:
```python
import functools

import jax
import jax.numpy as jnp
from jax import lax
from jax.experimental import pallas as pl
from jax.experimental.pallas import tpu as pltpu
from jax.sharding import PartitionSpec as P

X, Y, Z = 4, 4, 8
LIMIT = 44
R = 2
HALVES = ((0, 0), (1, 4), (0, 4), (1, 0), (2, 0), (2, 4))
F32, BF16 = jnp.float32, jnp.bfloat16


def kernel(hid, head, labels, loss_out, state_out, grad_out,
           w, wl, relay, wt, h, own, lab, e, errs, hs,
           stx, sty, stz, full, sb, ry, zs, rz, fs, fin,
           load_s, w_s, wl_r, rel_r, w2_r, b1_s, b1_r, lab_s, lab_r,
           hz_s, hz_r, hy_s, hy_r, hd_s, hd_r, hr_s, hr_r, rd_s, rd_r, e_s, e_r, eh_r,
           sx_s, sx_r, sy_s, sy_r, sz_s, sz_r,
           ry_s, ry_r, rz_s, rz_r, f_s, f_r, g_s):
    f, v = lax.axis_index("fsdp"), lax.axis_index("vocab")
    x, c = lax.div(f, 2), lax.rem(f, 2)
    y, z = lax.div(v, Z), lax.rem(v, Z)
    xp, xm, xo = lax.rem(x + 1, X), lax.rem(x + 3, X), lax.rem(x + 2, X)
    yp, ym, yo = lax.rem(y + 1, Y), lax.rem(y + 3, Y), lax.rem(y + 2, Y)
    fp, fm, fo, fq = 2 * xp + c, 2 * xm + c, 2 * xo + c, 2 * x + 1 - c
    ys = [lax.rem(y + k, Y) for k in range(Y)]
    zs_at = [lax.rem(z + k, Z) for k in range(Z)]
    xs = [x, xp, xo, xm]
    group = [[2 * a + d for d in range(2)] for a in xs]
    to_y = [{"fsdp": f, "vocab": Z * a + z} for a in ys]
    to_z = [{"fsdp": f, "vocab": Z * y + b} for b in zs_at]
    sends, calls, draining = [], {0: [], 1: []}, [False]
    role = [None]

    def only(core):
        def wrap(fn):
            def run(*args):
                calls[core].append((fn, args))

                @pl.when(c == core)
                def _():
                    role[0] = core
                    fn(*args)
                    role[0] = None
            run.__name__ = fn.__name__
            return run
        return wrap

    def at_f(g):
        return {"fsdp": g, "vocab": v}

    partner = at_f(fq)

    def send(src, dst, ssem, rsem, device):
        copy = pltpu.make_async_remote_copy(
            src_ref=src, dst_ref=dst, send_sem=ssem, recv_sem=rsem,
            device_id=device, device_id_type=pl.DeviceIdType.MESH)
        if draining[0]:
            copy.wait_send()
            return
        copy.start()
        if role[0] is None:
            sends.append(copy)

    def arrived(dst, rsem):
        if draining[0]:
            return
        pltpu.make_async_remote_copy(
            src_ref=dst, dst_ref=dst, send_sem=g_s.at[0], recv_sem=rsem,
            device_id=partner, device_id_type=pl.DeviceIdType.MESH).wait_recv()

    def home(t):
        return {"fsdp": 2 * t + lax.div(z, 4), "vocab": Z * x + 4 * c + y}

    def origin(r):
        return {"fsdp": 2 * y + lax.div(z, 4), "vocab": Z * lax.rem(z, 4) + 4 * c + r}

    own_home = jnp.logical_and(y == x, z == 4 * c + y)

    load_w = pltpu.make_async_copy(head, w, load_s.at[0])
    load_w.start()
    columns = pl.ds(pl.multiple_of(256 * f, 256), 256)
    load_own = pltpu.make_async_copy(head.at[:, columns], wl.at[f], load_s.at[1])
    load_own.start()

    barrier = pltpu.get_barrier_semaphore()

    def hello(device):
        pl.semaphore_signal(barrier, inc=1, device_id=device, device_id_type=pl.DeviceIdType.MESH)

    for k in range(1, 8):
        hello(at_f(lax.rem(f + k, 8)))
    for k in range(1, Y):
        hello(to_y[k])
    for k in range(1, Z):
        hello(to_z[k])
    for r in range(4):
        @pl.when(jnp.logical_not(jnp.logical_and(own_home, y == r)))
        def _():
            hello(origin(r))

    load_hid = pltpu.make_async_copy(hid, own, load_s.at[2])
    load_hid.start()
    load_lab = pltpu.make_async_copy(labels, lab.at[f, 0:1], load_s.at[3])
    load_lab.start()
    load_mine = pltpu.make_async_copy(hid, h.at[x, y, z, 1], load_s.at[4])

    @pl.when(c == 1)
    def _():
        load_mine.start()

    def begin():
        load_w.wait()
        load_hid.wait()
        load_lab.wait()

        @pl.when(c == 1)
        def _():
            load_mine.wait()

        pl.semaphore_wait(barrier, 7 + 3 + 7 + 4 - own_home.astype(jnp.int32))

    begin()

    for i in range(1, X):
        send(own, h.at[x, y, z, c], b1_s.at[i], b1_r.at[x, c], at_f(group[i][1]))

    def to_carrier():
        send(own, h.at[x, y, z, 0], b1_s.at[0], b1_r.at[x, 0], partner)

    to_carrier = only(0)(to_carrier)
    to_carrier()
    for k in range(1, 8):
        send(lab.at[f], lab.at[f], lab_s.at[k], lab_r.at[f], at_f(lax.rem(f + k, 8)))

    def cols(g):
        return pl.ds(pl.multiple_of(256 * g, 256), 256)

    for d in range(2):
        send(w.at[0:192, cols(2 * xo + d)], relay.at[0, c, d], w_s.at[d], rel_r.at[0, c, d], at_f(group[1][0]))
        send(w.at[192:384, cols(2 * xo + d)], relay.at[1, c, d], w_s.at[2 + d], rel_r.at[1, c, d], at_f(group[3][0]))
    send(w.at[:, cols(fq)], wl.at[f], w_s.at[4], wl_r.at[f], at_f(fq))
    for d in range(2):
        send(w.at[:, cols(2 * xp + d)], wl.at[f], w_s.at[5 + d], wl_r.at[f], at_f(2 * xp + d))
        send(w.at[:, cols(2 * xm + d)], wl.at[f], w_s.at[7 + d], wl_r.at[f], at_f(2 * xm + d))

    def head_in():
        load_own.wait()
        for g in (fq, 2 * xp, 2 * xp + 1, 2 * xm, 2 * xm + 1):
            arrived(wl.at[g], wl_r.at[g])
        for d in range(2):
            arrived(wl.at[2 * xo + d, 0:192], w2_r.at[0, d])
            arrived(wl.at[2 * xo + d, 192:384], w2_r.at[1, d])

    @only(0)
    def relays():
        for d in range(2):
            for o in range(2):
                arrived(relay.at[0, o, d], rel_r.at[0, o, d])
                send(relay.at[0, o, d], wl.at[group[3][o], 0:192],
                     w_s.at[9 + 2 * d + o], w2_r.at[0, o], at_f(group[1][d]))
                arrived(relay.at[1, o, d], rel_r.at[1, o, d])
                send(relay.at[1, o, d], wl.at[group[1][o], 192:384],
                     w_s.at[13 + 2 * d + o], w2_r.at[1, o], at_f(group[3][d]))

    def have(t):
        arrived(h.at[t, y, z, 0], b1_r.at[t, 0])

        @pl.when(x != t)
        def _():
            arrived(h.at[t, y, z, 1], b1_r.at[t, 1])

    @only(1)
    def hidden_z(t):
        have(t)
        block = h.at[t, y, z]
        for k in range(1, Z):
            send(block, block, hz_s.at[t, k], hz_r.at[t, k], to_z[k])

    @only(1)
    def ring_y():
        have(R)
        block = h.at[R, y, z]
        for k in range(1, Y):
            send(block, block, hz_s.at[R, k], hz_r.at[R, k], to_y[k])

    def ring_send(step):
        right, left = zs_at[(1 - step) % Z], zs_at[step - 1]
        low, high = ((0, 4), (0, 4)) if step < 4 else ((0, 2), (2, 4))
        block = h.at[R, low[0]:low[1], right]
        send(block, block, hr_s.at[0, step], hr_r.at[0, step], to_z[1])
        block = h.at[R, high[0]:high[1], left]
        send(block, block, hr_s.at[1, step], hr_r.at[1, step], to_z[7])

    def ring_partner(n, column):
        block = h.at[R, :, column]
        send(block, block, rd_s.at[n], rd_r.at[n], partner)

    @only(1)
    def ring_start():
        for k in range(1, Y):
            arrived(h.at[R, ys[Y - k], z], hz_r.at[R, k])
        ring_send(1)
        ring_partner(0, z)

    @only(1)
    def ring_next(step):
        left, right = zs_at[Z - step], zs_at[step]
        arrived(h.at[R, :, left], hr_r.at[0, step])
        arrived(h.at[R, :, right], hr_r.at[1, step])
        ring_send(step + 1)
        ring_partner(2 * step - 1, left)
        ring_partner(2 * step, right)

    @only(1)
    def ring_end():
        far = zs_at[4]
        arrived(h.at[R, 0:2, far], hr_r.at[0, 4])
        arrived(h.at[R, 2:4, far], hr_r.at[1, 4])
        ring_partner(7, far)

    def to_partner(t, row, low, n):
        block = h.at[t, row, low:low + (4 if n else Z)]
        send(block, block, hd_s.at[t, n], hd_r.at[t, n], partner)

    @only(1)
    def hidden_y(t):
        for k in range(1, Z):
            arrived(h.at[t, y, zs_at[Z - k]], hz_r.at[t, k])
        low, high = h.at[t, y, 0:4], h.at[t, y, 4:8]
        send(low, low, hy_s.at[t, 0], hy_r.at[t, 0], to_y[1])
        send(high, high, hy_s.at[t, 1], hy_r.at[t, 1], to_y[3])
        send(high, high, hy_s.at[t, 4], hy_r.at[t, 4], to_y[1])
        send(low, low, hy_s.at[t, 5], hy_r.at[t, 5], to_y[3])
        to_partner(t, y, 0, 0)

    @only(1)
    def hidden_y2(t):
        block = h.at[t, ym, 0:4]
        arrived(block, hy_r.at[t, 0])
        send(block, block, hy_s.at[t, 2], hy_r.at[t, 2], to_y[1])
        block = h.at[t, yp, 4:8]
        arrived(block, hy_r.at[t, 1])
        send(block, block, hy_s.at[t, 3], hy_r.at[t, 3], to_y[3])
        to_partner(t, ym, 0, 1)
        to_partner(t, yp, 4, 2)

    @only(1)
    def hidden_end(t):
        for n, (row, low) in enumerate(HALVES[2:]):
            row = (ym, yp, yo)[row]
            arrived(h.at[t, row, low:low + 4], hy_r.at[t, (4, 5, 2, 3)[n]])
            to_partner(t, row, low, 3 + n)

    @only(0)
    def hidden_all(t):
        if t == R:
            for n, k in enumerate((0, 7, 1, 6, 2, 5, 3, 4)):
                arrived(h.at[t, :, zs_at[k]], rd_r.at[n])
        else:
            arrived(h.at[t, y], hd_r.at[t, 0])
            for n, (row, low) in enumerate(HALVES):
                arrived(h.at[t, (ym, yp, yo)[row], low:low + 4], hd_r.at[t, 1 + n])

    hidden_z(0)
    hidden_z(3)
    hidden_z(1)
    ring_y()
    ring_start()
    hidden_y(0)
    relays()
    hidden_y2(0)
    hidden_y(3)
    ring_next(1)
    hidden_end(0)
    hidden_y2(3)
    hidden_y(1)
    head_in()
    for g in range(8):
        wt[:, 384 * g:384 * g + 384] = wl[g].T
    for k in range(1, 8):
        g = lax.rem(f + k, 8)
        arrived(lab.at[g], lab_r.at[g])

    def wanted(t):
        return jnp.concatenate([lab[2 * t, 0:1, :], lab[2 * t + 1, 0:1, :]], axis=1)

    def rows_of(g):
        return v * 2048 + g * 256 + lax.broadcasted_iota(jnp.int32, (256, 256), 0)

    def forward(t):
        hidden_all(t)
        states = jnp.concatenate(
            [h[t, :, :, 0].reshape(3072, 128), h[t, :, :, 1].reshape(3072, 128)], axis=1)
        logits = jnp.dot(wt[...], states, preferred_element_type=F32)
        peak = jnp.max(logits, axis=0, keepdims=True)
        shifted = jnp.exp(logits - peak)
        hits = rows_of(f) == wanted(t)
        stx[t, f, 0:1, :] = peak
        stx[t, f, 1:2, :] = jnp.sum(shifted, axis=0, keepdims=True)
        stx[t, f, 2:3, :] = jnp.sum(jnp.where(hits, logits, 0.0), axis=0, keepdims=True)
        e[t, f] = shifted.astype(BF16)
        for k in range(1, 8):
            g = lax.rem(f + k, 8)
            send(stx.at[t, f], stx.at[t, f], sx_s.at[t, k], sx_r.at[t, f], at_f(g))
        low, high, block = e.at[t, f, 0:128], e.at[t, f, 128:256], e.at[t, f]
        send(low, low, e_s.at[t, 0], eh_r.at[t, c, 2], at_f(group[1][0]))
        send(high, high, e_s.at[t, 1], eh_r.at[t, c, 3], at_f(group[3][0]))
        send(high, high, e_s.at[t, 2], eh_r.at[t, c, 4], at_f(group[1][0]))
        send(low, low, e_s.at[t, 3], eh_r.at[t, c, 5], at_f(group[3][0]))
        send(block, block, e_s.at[t, 4], e_r.at[t, f], partner)

    @only(0)
    def errors_2(t):
        for d in range(2):
            block = e.at[t, group[3][d], 0:128]
            arrived(block, eh_r.at[t, d, 2])
            send(block, block, e_s.at[t, 5 + d], eh_r.at[t, d, 0], at_f(group[1][0]))
            block = e.at[t, group[1][d], 128:256]
            arrived(block, eh_r.at[t, d, 3])
            send(block, block, e_s.at[t, 7 + d], eh_r.at[t, d, 1], at_f(group[3][0]))

    @only(0)
    def errors_3(t):
        for d in range(2):
            arrived(e.at[t, group[3][d], 128:256], eh_r.at[t, d, 4])
            arrived(e.at[t, group[1][d], 0:128], eh_r.at[t, d, 5])
            for i, a in enumerate((3, 1)):
                block = e.at[t, group[a][d]]
                send(block, block, e_s.at[t, 9 + 2 * d + i], e_r.at[t, group[a][d]], partner)
        for d in range(2):
            block = e.at[t, group[2][d]]
            arrived(e.at[t, group[2][d], 0:128], eh_r.at[t, d, 0])
            arrived(e.at[t, group[2][d], 128:256], eh_r.at[t, d, 1])
            send(block, block, e_s.at[t, 13 + d], e_r.at[t, group[2][d]], partner)

    @only(1)
    def errors_all(t):
        for a in (3, 1, 2):
            for d in range(2):
                arrived(e.at[t, group[a][d]], e_r.at[t, group[a][d]])

    def combine(ref, t, n):
        peaks = [ref[t, i, 0:1, :] for i in range(n)]
        peak = functools.reduce(jnp.maximum, peaks)
        total = sum(ref[t, i, 1:2, :] * jnp.exp(peaks[i] - peak) for i in range(n))
        target = sum(ref[t, i, 2:3, :] for i in range(n))
        return peak, total, target

    def put(ref, t, i, values):
        for row, value in enumerate(values):
            ref[t, i, row:row + 1, :] = value

    def stats_y(t):
        for k in range(1, 8):
            g = lax.rem(f + k, 8)
            arrived(stx.at[t, g], sx_r.at[t, g])
        put(sty, t, y, combine(stx, t, 8))
        for k in range(1, Y):
            send(sty.at[t, y], sty.at[t, y], sy_s.at[t, k], sy_r.at[t, k], to_y[k])

    def stats_z(t):
        for k in range(1, Y):
            arrived(sty.at[t, lax.rem(y + Y - k, Y)], sy_r.at[t, k])
        put(stz, t, z, combine(sty, t, Y))
        for k in range(1, Z):
            send(stz.at[t, z], stz.at[t, z], sz_s.at[t, k], sz_r.at[t, k], to_z[k])

    def backward(t):
        for k in range(1, Z):
            arrived(stz.at[t, lax.rem(z + Z - k, Z)], sz_r.at[t, k])
        peak, total, target = combine(stz, t, Z)
        full[t, 0:1, :] = jnp.log(total) + peak - target
        at_label = jnp.exp(target - peak) / total - 1.0
        arrived(e.at[t, fq], e_r.at[t, fq])
        errors_all(t)
        for g in range(8):
            scale = jnp.exp(stx[t, g, 0:1, :] - peak) / total
            value = e[t, g].astype(F32) * scale
            value = jnp.where(rows_of(g) == wanted(t), at_label, value)
            errs[g, :, 256 * t:256 * t + 256] = value.astype(BF16)
        terms = jnp.dot(w[...], errs[:, :, 256 * t:256 * t + 256].reshape(2048, 256),
                        preferred_element_type=F32)
        sb[t] = terms.reshape(4, 96, 256)
        for k in range(1, Y):
            a = lax.rem(y + k, Y)
            send(sb.at[t, a], ry.at[t, k - 1], ry_s.at[t, k - 1], ry_r.at[t, k - 1], to_y[k])

    def reduce_y(t):
        total = sb[t, y]
        for k in range(Y - 1):
            arrived(ry.at[t, k], ry_r.at[t, k])
            total = total + ry[t, k]
        for d in range(2):
            for r in range(4):
                zs[t, 4 * d + r] = total[24 * r:24 * r + 24, 128 * d:128 * d + 128]
        for k in range(1, Z):
            b = lax.rem(z + k, Z)
            send(zs.at[t, b], rz.at[t, k - 1], rz_s.at[t, k - 1], rz_r.at[t, k - 1], to_z[k])

    def home_copy(t):
        return pltpu.make_async_remote_copy(
            src_ref=fs.at[t], dst_ref=fin.at[lax.rem(z, 4)], send_sem=f_s.at[t], recv_sem=f_r.at[lax.rem(z, 4)],
            device_id=home(t), device_id_type=pl.DeviceIdType.MESH)

    def reduce_z(t):
        total = zs[t, z]
        for k in range(Z - 1):
            arrived(rz.at[t, k], rz_r.at[t, k])
            total = total + rz[t, k]
        fs[t] = total
        stays = jnp.logical_and(own_home, x == t)

        @pl.when(stays)
        def _():
            fin[lax.rem(z, 4)] = fs[t]

        @pl.when(jnp.logical_not(stays))
        def _():
            home_copy(t).start()

    forward(0)
    ring_next(2)
    hidden_end(3)
    forward(3)
    errors_2(0)
    stats_y(0)
    hidden_y2(1)
    ring_next(3)
    stats_z(0)
    ring_end()
    forward(2)
    errors_2(3)
    stats_y(3)
    errors_3(0)
    hidden_end(1)
    forward(1)
    backward(0)
    errors_2(2)
    stats_z(3)
    stats_y(2)
    errors_3(3)
    stats_y(1)
    errors_2(1)
    stats_z(2)
    backward(3)
    stats_z(1)
    reduce_y(0)
    errors_3(2)
    errors_3(1)
    backward(2)
    backward(1)
    reduce_y(3)
    reduce_z(0)

    for t in range(X):
        for d in range(2):
            hs[:, 256 * t + 128 * d:256 * t + 128 * d + 128] = h[t, x, pl.ds(4 * c, 4), d].reshape(384, 128)
    for g in range(8):
        grad_out[:, 256 * g:256 * g + 256] = lax.dot_general(
            hs[...], errs[g], (((1,), (1,)), ((), ())), preferred_element_type=F32)
        if g == 1:
            reduce_y(2)
        if g == 3:
            reduce_z(3)
    reduce_y(1)
    reduce_z(2)

    def drain():
        for copy in sends:
            copy.wait_send()
        draining[0] = True
        for core in range(2):
            @pl.when(c == core)
            def _():
                for fn, args in calls[core]:
                    fn(*args)
        draining[0] = False

    drain()
    losses = full[x, 0:1, :]
    loss_out[...] = jnp.where(c == 0, losses[:, 0:128], losses[:, 128:256])
    reduce_z(1)
    for r in range(4):
        @pl.when(jnp.logical_not(jnp.logical_and(own_home, y == r)))
        def _():
            arrived(fin.at[r], f_r.at[r])
    state_out[...] = fin[...].reshape(96, 128).astype(BF16)
    for t in range(X):
        @pl.when(jnp.logical_not(jnp.logical_and(own_home, x == t)))
        def _():
            home_copy(t).wait_send()


def local(hidden_states, head, labels):
    dma = pltpu.SemaphoreType.DMA
    vmem = pltpu.VMEM
    loss, state, grad = pl.pallas_call(
        kernel,
        name="head_loss",
        out_shape=(
            jax.ShapeDtypeStruct((1, 128), F32),
            jax.ShapeDtypeStruct((96, 128), BF16),
            jax.ShapeDtypeStruct((384, 2048), F32),
        ),
        in_specs=[pl.BlockSpec(memory_space=pltpu.HBM)] * 3,
        out_specs=(
            pl.BlockSpec(memory_space=vmem),
            pl.BlockSpec(memory_space=vmem),
            pl.BlockSpec(memory_space=vmem),
        ),
        scratch_shapes=[
            vmem((384, 2048), BF16),
            vmem((8, 384, 256), BF16),
            vmem((2, 2, 2, 192, 256), BF16),
            vmem((256, 3072), BF16),
            vmem((X, Y, Z, 2, 96, 128), BF16),
            vmem((96, 128), BF16),
            vmem((8, 8, 128), jnp.int32),
            vmem((X, 8, 256, 256), BF16),
            vmem((8, 256, 1024), BF16),
            vmem((384, 1024), BF16),
            vmem((X, 8, 8, 256), F32),
            vmem((X, Y, 8, 256), F32),
            vmem((X, Z, 8, 256), F32),
            vmem((X, 8, 256), F32),
            vmem((X, 4, 96, 256), F32),
            vmem((X, Y - 1, 96, 256), F32),
            vmem((X, Z, 24, 128), F32),
            vmem((X, Z - 1, 24, 128), F32),
            vmem((X, 24, 128), F32),
            vmem((4, 24, 128), F32),
            dma((5,)), dma((17,)), dma((8,)), dma((2, 2, 2)), dma((2, 2)),
            dma((X,)), dma((X, 2)), dma((8,)), dma((8,)),
            dma((X, Z)), dma((X, Z)), dma((X, 6)), dma((X, 6)), dma((X, 7)), dma((X, 7)),
            dma((2, 5)), dma((2, 5)), dma((8,)), dma((8,)),
            dma((X, 15)), dma((X, 8)), dma((X, 2, 6)),
            dma((X, 8)), dma((X, 8)), dma((X, Y)), dma((X, Y)), dma((X, Z)), dma((X, Z)),
            dma((X, Y - 1)), dma((X, Y - 1)), dma((X, Z - 1)), dma((X, Z - 1)),
            dma((X,)), dma((4,)), dma((1,)),
        ],
        compiler_params=pltpu.CompilerParams(
            collective_id=0, has_side_effects=True, vmem_limit_bytes=LIMIT * 1024 * 1024),
    )(*(pltpu.with_memory_space_constraint(a, pltpu.HBM)
        for a in (hidden_states.T, head, labels.reshape(1, 128))))
    return (loss.reshape(128), state.T, grad)


def solution(mesh):
    in_specs = (P("fsdp", "vocab"), P("fsdp", "vocab"), P("fsdp"))
    out_specs = (P("fsdp"), P("fsdp", "vocab"), P("fsdp", "vocab"))
    return jax.shard_map(local, mesh=mesh, in_specs=in_specs, out_specs=out_specs, check_vma=False)
```

time: 95.6 us -> 92.7 us (0.970)
  the two profiles are of different devices: /device:TPU:7 before, /device:TPU:26 now
where the time goes in v4:
time: 92.7 us; the launch traced here: 92.6 us
  Pallas kernels  89.1 us (96%)
  local copies, waits for them, and re-layouts  2.78 us (3%)
    pallas_call x1, Pallas kernels, local(): pl.pallas_call(kernel, name='head_loss', out_shape=(jax.ShapeDtypeStruct(...  89.1 us
    unnamed x3, local copies, waits for them, and re-layouts  2.78 us

profile of v4, /device:TPU:26, one launch (start us, length us, event | category | flops | bytes accessed | tf_op | source)
XLA Modules:
  0.0 92.6 jit_solution(10684687673984976487)
XLA Ops:
  0.6 89.1 %head_loss.1 = (f32[1,128]{1,0:T(1,128)S(1)}, bf16[96,128]{1,0:T(8,128)(2,1)S(1)}, f32[384,2048]{1,0:T(8,128)S(1)}) custom-call(bf16[96,128]{1,0:T(8,128)(2,1)} %bitcast.6, bf16[384,2048]{1,0:T(8,128)(2,1)} %head.1, s32[1,128]{1,0:T(1,128)} %bitcast.7), custom_call_target="tpu_custom_call" | custom-call | tf_op jit(solution)/shard_map/head_loss/pallas_call | solution.py:502
  89.8 0.5 copy.9
  90.3 0.6 copy.10
  90.9 1.7 %copy.11 = f32[384,2048]{1,0:T(8,128)} copy(f32[384,2048]{1,0:T(8,128)S(1)} %get-tuple-element.14) | data formatting | bytes 6291456

commit v5 on v4

--- a/solution.py
+++ b/solution.py
@@ -16,7 +16,7 @@
 
 def kernel(hid, head, labels, loss_out, state_out, grad_out,
            w, wl, relay, wt, h, own, lab, e, errs, hs,
-           stx, sty, stz, full, sb, ry, zs, rz, fs, fin,
+           stx, sty, stz, full, sb, ry, rm, zs, rz, fs, fin,
            load_s, w_s, wl_r, rel_r, w2_r, b1_s, b1_r, lab_s, lab_r,
            hz_s, hz_r, hy_s, hy_r, hd_s, hd_r, hr_s, hr_r, rd_s, rd_r, e_s, e_r, eh_r,
            sx_s, sx_r, sy_s, sy_r, sz_s, sz_r,
@@ -386,15 +386,26 @@
         terms = jnp.dot(w[...], errs[:, :, 256 * t:256 * t + 256].reshape(2048, 256),
                         preferred_element_type=F32)
         sb[t] = terms.reshape(4, 96, 256)
-        for k in range(1, Y):
-            a = lax.rem(y + k, Y)
-            send(sb.at[t, a], ry.at[t, k - 1], ry_s.at[t, k - 1], ry_r.at[t, k - 1], to_y[k])
+        send(sb.at[t, yo, 0:48], rm.at[t, 0], ry_s.at[t, 0], ry_r.at[t, 0], to_y[1])
+        send(sb.at[t, yo, 48:96], rm.at[t, 1], ry_s.at[t, 1], ry_r.at[t, 1], to_y[3])
+        send(sb.at[t, yp, 48:96], ry.at[t, 0, 48:96], ry_s.at[t, 2], ry_r.at[t, 2], to_y[1])
+        send(sb.at[t, ym, 0:48], ry.at[t, 1, 0:48], ry_s.at[t, 3], ry_r.at[t, 3], to_y[3])
+
+    def join_y(t):
+        arrived(rm.at[t, 0], ry_r.at[t, 0])
+        rm[t, 2] = sb[t, yp, 0:48] + rm[t, 0]
+        send(rm.at[t, 2], ry.at[t, 0, 0:48], ry_s.at[t, 4], ry_r.at[t, 4], to_y[1])
+        arrived(rm.at[t, 1], ry_r.at[t, 1])
+        rm[t, 3] = sb[t, ym, 48:96] + rm[t, 1]
+        send(rm.at[t, 3], ry.at[t, 1, 48:96], ry_s.at[t, 5], ry_r.at[t, 5], to_y[3])
 
     def reduce_y(t):
         total = sb[t, y]
-        for k in range(Y - 1):
-            arrived(ry.at[t, k], ry_r.at[t, k])
-            total = total + ry[t, k]
+        arrived(ry.at[t, 0, 48:96], ry_r.at[t, 2])
+        arrived(ry.at[t, 1, 0:48], ry_r.at[t, 3])
+        arrived(ry.at[t, 0, 0:48], ry_r.at[t, 4])
+        arrived(ry.at[t, 1, 48:96], ry_r.at[t, 5])
+        total = total + ry[t, 0] + ry[t, 1]
         for d in range(2):
             for r in range(4):
                 zs[t, 4 * d + r] = total[24 * r:24 * r + 24, 128 * d:128 * d + 128]
@@ -443,6 +454,7 @@
     errors_2(2)
     stats_z(3)
     stats_y(2)
+    join_y(0)
     errors_3(3)
     stats_y(1)
     errors_2(1)
@@ -452,10 +464,11 @@
     reduce_y(0)
     errors_3(2)
     errors_3(1)
+    join_y(3)
     backward(2)
     backward(1)
+    join_y(2)
     reduce_y(3)
-    reduce_z(0)
 
     for t in range(X):
         for d in range(2):
@@ -463,10 +476,12 @@
     for g in range(8):
         grad_out[:, 256 * g:256 * g + 256] = lax.dot_general(
             hs[...], errs[g], (((1,), (1,)), ((), ())), preferred_element_type=F32)
-        if g == 1:
+        if g == 3:
+            join_y(1)
+            reduce_z(0)
+        if g == 5:
             reduce_y(2)
-        if g == 3:
-            reduce_z(3)
+    reduce_z(3)
     reduce_y(1)
     reduce_z(2)
 
@@ -529,7 +544,8 @@
             vmem((X, Z, 8, 256), F32),
             vmem((X, 8, 256), F32),
             vmem((X, 4, 96, 256), F32),
-            vmem((X, Y - 1, 96, 256), F32),
+            vmem((X, 2, 96, 256), F32),
+            vmem((X, 4, 48, 256), F32),
             vmem((X, Z, 24, 128), F32),
             vmem((X, Z - 1, 24, 128), F32),
             vmem((X, 24, 128), F32),
@@ -540,7 +556,7 @@
             dma((2, 5)), dma((2, 5)), dma((8,)), dma((8,)),
             dma((X, 15)), dma((X, 8)), dma((X, 2, 6)),
             dma((X, 8)), dma((X, 8)), dma((X, Y)), dma((X, Y)), dma((X, Z)), dma((X, Z)),
-            dma((X, Y - 1)), dma((X, Y - 1)), dma((X, Z - 1)), dma((X, Z - 1)),
+            dma((X, 6)), dma((X, 6)), dma((X, Z - 1)), dma((X, Z - 1)),
             dma((X,)), dma((4,)), dma((1,)),
         ],
         compiler_params=pltpu.CompilerParams(

time: 92.7 us -> 91 us (0.982); the launches traced: 92.6 us -> 89.9 us
  Pallas kernels: 89.1 us -> 86.4 us
    pallas_call x1, Pallas kernels: 89.1 us -> 86.4 us  [local(): pl.pallas_call(kernel, name='head_loss', out_shape=(jax.ShapeDtypeStruct(...]
where the time goes in v5:
time: 91 us; the launch traced here: 89.9 us
  Pallas kernels  86.4 us (95%)
  local copies, waits for them, and re-layouts  2.78 us (3%)
    pallas_call x1, Pallas kernels, local(): pl.pallas_call(kernel, name='head_loss', out_shape=(jax.ShapeDtypeStruct(...  86.4 us
    unnamed x3, local copies, waits for them, and re-layouts  2.78 us

profile of v5, /device:TPU:26, one launch (start us, length us, event | category | flops | bytes accessed | tf_op | source)
XLA Modules:
  0.0 89.9 jit_solution(5631333009684278239)
XLA Ops:
  0.6 86.4 %head_loss.1 = (f32[1,128]{1,0:T(1,128)S(1)}, bf16[96,128]{1,0:T(8,128)(2,1)S(1)}, f32[384,2048]{1,0:T(8,128)S(1)}) custom-call(bf16[96,128]{1,0:T(8,128)(2,1)} %bitcast.6, bf16[384,2048]{1,0:T(8,128)(2,1)} %head.1, s32[1,128]{1,0:T(1,128)} %bitcast.7), custom_call_target="tpu_custom_call" | custom-call | tf_op jit(solution)/shard_map/head_loss/pallas_call | solution.py:517
  87.1 0.5 copy.9
  87.6 0.6 copy.10
  88.2 1.7 %copy.11 = f32[384,2048]{1,0:T(8,128)} copy(f32[384,2048]{1,0:T(8,128)S(1)} %get-tuple-element.14) | data formatting | bytes 6291456

commit v6 on v5

--- a/solution.py
+++ b/solution.py
@@ -10,6 +10,7 @@
 X, Y, Z = 4, 4, 8
 LIMIT = 44
 R = 2
+FAR_Z, FAR_Y = (4, 3, 5, 2, 6, 1, 7), (2, 1, 3)
 HALVES = ((0, 0), (1, 4), (0, 4), (1, 0), (2, 0), (2, 4))
 F32, BF16 = jnp.float32, jnp.bfloat16
 
@@ -94,9 +95,9 @@
 
     for k in range(1, 8):
         hello(at_f(lax.rem(f + k, 8)))
-    for k in range(1, Y):
+    for k in FAR_Y:
         hello(to_y[k])
-    for k in range(1, Z):
+    for k in FAR_Z:
         hello(to_z[k])
     for r in range(4):
         @pl.when(jnp.logical_not(jnp.logical_and(own_home, y == r)))
@@ -178,14 +179,14 @@
     def hidden_z(t):
         have(t)
         block = h.at[t, y, z]
-        for k in range(1, Z):
+        for k in FAR_Z:
             send(block, block, hz_s.at[t, k], hz_r.at[t, k], to_z[k])
 
     @only(1)
     def ring_y():
         have(R)
         block = h.at[R, y, z]
-        for k in range(1, Y):
+        for k in FAR_Y:
             send(block, block, hz_s.at[R, k], hz_r.at[R, k], to_y[k])
 
     def ring_send(step):
@@ -360,14 +361,14 @@
             g = lax.rem(f + k, 8)
             arrived(stx.at[t, g], sx_r.at[t, g])
         put(sty, t, y, combine(stx, t, 8))
-        for k in range(1, Y):
+        for k in FAR_Y:
             send(sty.at[t, y], sty.at[t, y], sy_s.at[t, k], sy_r.at[t, k], to_y[k])
 
     def stats_z(t):
         for k in range(1, Y):
             arrived(sty.at[t, lax.rem(y + Y - k, Y)], sy_r.at[t, k])
         put(stz, t, z, combine(sty, t, Y))
-        for k in range(1, Z):
+        for k in FAR_Z:
             send(stz.at[t, z], stz.at[t, z], sz_s.at[t, k], sz_r.at[t, k], to_z[k])
 
     def backward(t):
@@ -409,7 +410,7 @@
         for d in range(2):
             for r in range(4):
                 zs[t, 4 * d + r] = total[24 * r:24 * r + 24, 128 * d:128 * d + 128]
-        for k in range(1, Z):
+        for k in FAR_Z:
             b = lax.rem(z + k, Z)
             send(zs.at[t, b], rz.at[t, k - 1], rz_s.at[t, k - 1], rz_r.at[t, k - 1], to_z[k])
 

time: 91 us -> 90.4 us (level)
  no operation moved by 1% of the time
where the time goes in v6:
time: 90.4 us; the launch traced here: 89 us
  Pallas kernels  85.5 us (95%)
  local copies, waits for them, and re-layouts  2.78 us (3%)
    pallas_call x1, Pallas kernels, local(): pl.pallas_call(kernel, name='head_loss', out_shape=(jax.ShapeDtypeStruct(...  85.5 us
    unnamed x3, local copies, waits for them, and re-layouts  2.78 us

profile of v6, /device:TPU:26, one launch (start us, length us, event | category | flops | bytes accessed | tf_op | source)
XLA Modules:
  0.0 89.0 jit_solution(8191349138389079342)
XLA Ops:
  0.6 85.5 %head_loss.1 = (f32[1,128]{1,0:T(1,128)S(1)}, bf16[96,128]{1,0:T(8,128)(2,1)S(1)}, f32[384,2048]{1,0:T(8,128)S(1)}) custom-call(bf16[96,128]{1,0:T(8,128)(2,1)} %bitcast.6, bf16[384,2048]{1,0:T(8,128)(2,1)} %head.1, s32[1,128]{1,0:T(1,128)} %bitcast.7), custom_call_target="tpu_custom_call" | custom-call | tf_op jit(solution)/shard_map/head_loss/pallas_call | solution.py:518
  86.2 0.5 copy.9
  86.7 0.6 copy.10
  87.3 1.7 %copy.11 = f32[384,2048]{1,0:T(8,128)} copy(f32[384,2048]{1,0:T(8,128)S(1)} %get-tuple-element.14) | data formatting | bytes 6291456
